TPU v7x, 8 devices: a whole 2x2x1 slice. The times are simulated.
8 devices in a mesh: dp: 1 (over z), seq: 8 (over y, x, core).
Axes of the slice: x: 2, y: 2, z: 1, core: 2. Of those that a mesh axis runs over, the one named last changes fastest.
Arguments:
- enc_out: bfloat16 [64, 16, 640], P('dp', 'seq')
- pred_out: bfloat16 [64, 8, 640], P('dp')
- w_enc: bfloat16 [640, 640], replicated
- w_pred: bfloat16 [640, 640], replicated
- w_out: bfloat16 [640, 4096], replicated
- labels: int32 [64, 7], P('dp')
- frame_len: int32 [64], P('dp')
- label_len: int32 [64], P('dp')
Outputs:
- output 1: float32 [64], P('dp')
- output 2: bfloat16 [64, 16, 640], P('dp', 'seq')
- output 3: float32 [640, 640], P('dp')
- output 4: float32 [640, 640], P('dp')
- output 5: float32 [640, 4096], P('dp')
All inputs are finite; a program needn't handle non-finite values.
Results may differ from a plain program's by a relative error of at most 0.0134743.
Values are sent between devices in bfloat16 or wider.
A program may use at most 1 GiB of HBM per device.

v0:
```python
import jax
import jax.numpy as jnp
from jax import lax
from jax.sharding import PartitionSpec as P

NEG_FILL = -1.0e30


def label_prefix(lab_lp):
    zero_col = jnp.zeros_like(lab_lp[:, :1])
    return jnp.concatenate([zero_col, jnp.cumsum(lab_lp[:, :-1], axis=1)], axis=1)


def label_weights(labels, w_out):
    n_utt = labels.shape[0]
    lab_ids = jnp.concatenate([labels, jnp.full((n_utt, 1), -1, jnp.int32)], axis=1)
    onehot = (lab_ids[:, :, None] == lax.broadcasted_iota(jnp.int32, (1, 1, w_out.shape[1]), 2)).astype(jnp.bfloat16)
    lab_w = jnp.einsum('buv,jv->buj', onehot, w_out, preferred_element_type=jnp.float32).astype(jnp.bfloat16)
    return lab_ids, lab_w


def joint_lattice(enc_blk, act_g, lab_w, w_enc, w_out):
    act_f = jnp.einsum('bth,hj->btj', enc_blk, w_enc, preferred_element_type=jnp.float32).astype(jnp.bfloat16)
    hidden = jnp.tanh(act_f[:, :, None, :].astype(jnp.float32) + act_g[:, None, :, :].astype(jnp.float32)).astype(jnp.bfloat16)
    logits = jnp.einsum('btuj,jv->btuv', hidden, w_out, preferred_element_type=jnp.float32)
    log_norm = jax.nn.logsumexp(logits, axis=-1)
    soft_probs = jnp.exp(logits - log_norm[..., None])
    blank_lp = logits[..., 0] - log_norm
    lab_lp = jnp.einsum('btuj,buj->btu', hidden, lab_w, preferred_element_type=jnp.float32) - log_norm
    return hidden, soft_probs, blank_lp, lab_lp


def alpha_rows(x_in, blank_lp, lab_lp):
    def frame_step(x_prev, frame_in):
        frame_blank, frame_lab = frame_in
        lab_sum = label_prefix(frame_lab)
        alpha_t = lab_sum + lax.cumlogsumexp(x_prev - lab_sum, axis=1)
        return alpha_t + frame_blank, alpha_t
    x_out, alphas = lax.scan(frame_step, x_in, (jnp.swapaxes(blank_lp, 0, 1), jnp.swapaxes(lab_lp, 0, 1)))
    return x_out, jnp.swapaxes(alphas, 0, 1)


def beta_rows(next_in, blank_lp, lab_lp, frame_ids, frame_len, boundary):
    def frame_step(next_row, frame_in):
        frame_blank, frame_lab, frame_id = frame_in
        lab_sum = label_prefix(frame_lab)
        beta_row = lax.cumlogsumexp(next_row + frame_blank + lab_sum, axis=1, reverse=True) - lab_sum
        beta_row = jnp.where((frame_id >= frame_len)[:, None], boundary, beta_row)
        return beta_row, (beta_row, next_row)
    first_row, (betas, beta_next) = lax.scan(frame_step, next_in, (jnp.swapaxes(blank_lp, 0, 1), jnp.swapaxes(lab_lp, 0, 1), frame_ids), reverse=True)
    return first_row, jnp.swapaxes(betas, 0, 1), jnp.swapaxes(beta_next, 0, 1)


def occupancy(alphas, betas, beta_next, blank_lp, lab_lp, log_prob, frame_ok):
    beta_up = jnp.concatenate([betas[:, :, 1:], jnp.full_like(betas[:, :, :1], NEG_FILL)], axis=2)
    norm_shift = log_prob[:, None, None]
    occ_blank = jnp.where(frame_ok, jnp.exp(jnp.minimum(alphas + blank_lp + beta_next - norm_shift, 0.0)), 0.0)
    occ_lab = jnp.where(frame_ok, jnp.exp(jnp.minimum(alphas + lab_lp + beta_up - norm_shift, 0.0)), 0.0)
    return occ_blank, occ_lab


def joint_backward(enc_blk, hidden, soft_probs, occ_blank, occ_lab, lab_ids, w_enc, w_out):
    vocab_ids = lax.broadcasted_iota(jnp.int32, (1, 1, 1, soft_probs.shape[-1]), 3)
    d_logits = (soft_probs * (occ_blank + occ_lab)[..., None] - jnp.where(vocab_ids == 0, occ_blank[..., None], 0.0) - jnp.where(vocab_ids == lab_ids[:, None, :, None], occ_lab[..., None], 0.0)).astype(jnp.bfloat16)
    d_hidden = jnp.einsum('btuv,jv->btuj', d_logits, w_out, preferred_element_type=jnp.float32)
    d_pre = (d_hidden * (1.0 - jnp.square(hidden.astype(jnp.float32)))).astype(jnp.bfloat16)
    d_act_f = jnp.sum(d_pre, axis=2, dtype=jnp.float32).astype(jnp.bfloat16)
    d_act_g = jnp.sum(d_pre, axis=1, dtype=jnp.float32)
    grad_enc = jnp.einsum('btj,hj->bth', d_act_f, w_enc, preferred_element_type=jnp.float32).astype(jnp.bfloat16)
    gw_enc = jnp.einsum('bth,btj->hj', enc_blk, d_act_f, preferred_element_type=jnp.float32)
    gw_out = jnp.einsum('btuj,btuv->jv', hidden, d_logits, preferred_element_type=jnp.float32)
    return grad_enc, gw_enc, gw_out, d_act_g


def solution(mesh):
    seq_size = mesh.shape['seq']
    fwd_pairs = [(src, src + 1) for src in range(seq_size - 1)]
    bwd_pairs = [(src + 1, src) for src in range(seq_size - 1)]

    def local_fn(enc_out, pred_out, w_enc, w_pred, w_out, labels, frame_len, label_len):
        seq_idx = lax.axis_index('seq')
        n_utt, n_loc, _ = enc_out.shape
        lab_pos = pred_out.shape[1]
        lab_ids, lab_w = label_weights(labels, w_out)
        act_g = jnp.einsum('buh,hj->buj', pred_out, w_pred, preferred_element_type=jnp.float32).astype(jnp.bfloat16)
        hidden, soft_probs, blank_lp, lab_lp = joint_lattice(enc_out, act_g, lab_w, w_enc, w_out)
        pos_ids = lax.broadcasted_iota(jnp.int32, (n_utt, lab_pos), 1)
        neg_rows = jnp.full((n_utt, lab_pos), NEG_FILL, jnp.float32)
        init_x = jnp.where(pos_ids == 0, 0.0, neg_rows)
        boundary = jnp.where(pos_ids == label_len[:, None], 0.0, neg_rows)
        frame_ids = seq_idx * n_loc + jnp.arange(n_loc, dtype=jnp.int32)

        def alpha_hop(hop_idx, x_in):
            x_out, _ = alpha_rows(x_in, blank_lp, lab_lp)
            received = lax.ppermute(x_out, 'seq', fwd_pairs)
            return jnp.where(seq_idx == 0, init_x, received)

        x_in = lax.fori_loop(0, seq_size - 1, alpha_hop, init_x)
        _, alphas = alpha_rows(x_in, blank_lp, lab_lp)

        def beta_hop(hop_idx, next_in):
            first_row, _, _ = beta_rows(next_in, blank_lp, lab_lp, frame_ids, frame_len, boundary)
            received = lax.ppermute(first_row, 'seq', bwd_pairs)
            return jnp.where(seq_idx == seq_size - 1, boundary, received)

        next_in = lax.fori_loop(0, seq_size - 1, beta_hop, boundary)
        first_row, betas, beta_next = beta_rows(next_in, blank_lp, lab_lp, frame_ids, frame_len, boundary)
        log_prob = lax.psum(jnp.where(seq_idx == 0, first_row[:, 0], 0.0), 'seq')
        frame_ok = (frame_ids[None, :] < frame_len[:, None])[:, :, None]
        occ_blank, occ_lab = occupancy(alphas, betas, beta_next, blank_lp, lab_lp, log_prob, frame_ok)
        grad_enc, gw_enc, gw_out, d_act_g = joint_backward(enc_out, hidden, soft_probs, occ_blank, occ_lab, lab_ids, w_enc, w_out)
        gw_pred = jnp.einsum('buh,buj->hj', pred_out, d_act_g, preferred_element_type=jnp.float32)
        gw_enc, gw_pred, gw_out = lax.psum((gw_enc, gw_pred, gw_out), 'seq')
        return -log_prob, grad_enc, gw_enc, gw_pred, gw_out

    in_specs = (P('dp', 'seq', None), P('dp', None, None), P(None, None), P(None, None), P(None, None), P('dp', None), P('dp'), P('dp'))
    out_specs = (P('dp'), P('dp', 'seq', None), P('dp', None), P('dp', None), P('dp', None))
    return jax.shard_map(local_fn, mesh=mesh, in_specs=in_specs, out_specs=out_specs, check_vma=False)
```

profile of v0, /device:TPU:0, one launch (start us, length us, event | category | flops | bytes accessed | tf_op | source)
XLA Modules:
  0.0 413.5 jit_solution(12659203330774211697)
XLA Ops:
  11.9 7.0 %fusion.56 = (f32[64,2,8]{2,1,0:T(2,128)S(1)}, f32[64,2,8,4096]{3,2,1,0:T(8,128)S(1)}) fusion(bf16[64,2,8,640]{3,2,1,0:T(8,128)(2,1)S(1)} %tanh_convert_fusion, bf16[640,4096]{1,0:T(8,128)(2,1)S(1)} %copy-done.10), kind=kOutput, calls=%fused_computation.92 | convolution fusion | flops 5372902400 | bytes 23334912 | tf_op jit(solution)/shard_map/btuj,jv->btuv/dot_general | solution.py:25
  18.9 5.7 %copy-done.2 = f32[64,2,8,4096]{3,2,1,0:T(8,128)} copy-done((f32[64,2,8,4096]{3,2,1,0:T(8,128)}, f32[64,2,8,4096]{3,2,1,0:T(8,128)S(1)}, u32[]{:S(2)}) %copy-start.2) | copy-done | bytes 16777240
  24.7 8.1 %exponential_reduce_fusion = f32[64,2,8]{2,1,0:T(2,128)S(1)} fusion(f32[64,2,8,4096]{3,2,1,0:T(8,128)} %copy-done.2, f32[64,2,8]{2,1,0:T(2,128)S(1)} %is-finite_select_fusion.1), kind=kLoop, calls=%fused_computation.31 | loop fusion | flops 8387584 | bytes 16785408 | tf_op jit(solution)/shard_map/reduce_sum | solution.py:26
  33.0 6.4 %fusion.27 = bf16[64,8,640,1]{2,1,0,3:T(8,128)(2,1)S(1)} fusion(bf16[640,4096]{1,0:T(8,128)(2,1)} %param.24, s32[64,8]{1,0:T(8,128)S(1)} %concatenate.18.clone), kind=kOutput, calls=%fused_computation.53 | convolution fusion | flops 2686779392 | bytes 5900288 | tf_op jit(solution)/shard_map/buv,jv->buj/dot_general | solution.py:18
  39.4 3.1 fusion.24
  45.7 37.5 %while.108 = (s32[]{:T(128)}, f32[64,8]{0,1:T(8,128)S(1)}, pred[]{:T(512)}, f32[64,2,8]{0,2,1:T(8,128)S(1)}, f32[64,2,8]{0,2,1:T(8,128)S(1)}, /*index=5*/f32[8]{...) while((s32[]{:T(128)}, f32[64,8]{0,1:T(8,128)S(1)}, ...), condition=%wide.region_18.19_spmd.clone, body=%wide.region_13.18_spmd.clone.sunk | while | flops 33412 | bytes 38227 | solution.py:98
  50.3 4.4 %collective-permute-start = (f32[64,8]{0,1:T(8,128)S(1)}, f32[64,8]{0,1:T(8,128)S(1)}, u32[]{:S(2)}, u32[]{:S(2)}) collective-permute-start(f32[64,8]{0,1:T(8,128)S(1)} %get-tuple-element.1120), channel_id=1, source_target_pairs={{0,1},{1,2},{2,3},{3,4},{4,5},{5,6},{6,7}} | collective-permute-start | bytes 6152 | tf_op jit(solution)/shard_map/while/body/eval_jaxpr/ppermute | solution.py:95
  56.1 4.1 collective-permute-start
  61.6 4.1 collective-permute-start
  67.1 4.1 collective-permute-start
  72.6 4.1 collective-permute-start
  78.1 4.1 collective-permute-start
  83.9 64.5 %while.105 = (s32[]{:T(128)}, f32[64,8]{0,1:T(8,128)S(1)}, pred[]{:T(512)}, f32[64,2,8]{0,2,1:T(8,128)S(1)}, f32[64,2,8]{0,2,1:T(8,128)S(1)}, /*index=5*/s32[64]...) while((s32[]{:T(128)}, f32[64,8]{0,1:T(8,128)S(1)}, ...), condition=%wide.region_7.8_spmd.clone, body=%wide.region_2.7_spmd.clone.sunk | while | flops 36039 | bytes 43299 | solution.py:106
  84.0 3.3 while.109
  88.5 4.2 %collective-permute-done.1 = f32[64,8]{0,1:T(8,128)S(1)} collective-permute-done((f32[64,8]{0,1:T(8,128)S(1)}, f32[64,8]{0,1:T(8,128)S(1)}, u32[]{:S(2)}, u32[]{:S(2)}) %collective-permute-start.1) | collective-permute-done | bytes 2080 | tf_op jit(solution)/shard_map/while/body/eval_jaxpr/ppermute | solution.py:103
  92.7 3.3 while.109
  97.3 5.1 %collective-permute-done.1 = f32[64,8]{0,1:T(8,128)S(1)} collective-permute-done((f32[64,8]{0,1:T(8,128)S(1)}, f32[64,8]{0,1:T(8,128)S(1)}, u32[]{:S(2)}, u32[]{:S(2)}) %collective-permute-start.1) | collective-permute-done | bytes 2080 | tf_op jit(solution)/shard_map/while/body/eval_jaxpr/ppermute | solution.py:103
  102.4 3.3 while.109
  107.0 4.4 %collective-permute-done.1 = f32[64,8]{0,1:T(8,128)S(1)} collective-permute-done((f32[64,8]{0,1:T(8,128)S(1)}, f32[64,8]{0,1:T(8,128)S(1)}, u32[]{:S(2)}, u32[]{:S(2)}) %collective-permute-start.1) | collective-permute-done | bytes 2080 | tf_op jit(solution)/shard_map/while/body/eval_jaxpr/ppermute | solution.py:103
  111.4 3.3 while.109
  115.9 5.1 %collective-permute-done.1 = f32[64,8]{0,1:T(8,128)S(1)} collective-permute-done((f32[64,8]{0,1:T(8,128)S(1)}, f32[64,8]{0,1:T(8,128)S(1)}, u32[]{:S(2)}, u32[]{:S(2)}) %collective-permute-start.1) | collective-permute-done | bytes 2080 | tf_op jit(solution)/shard_map/while/body/eval_jaxpr/ppermute | solution.py:103
  121.0 3.3 while.109
  125.6 4.5 %collective-permute-done.1 = f32[64,8]{0,1:T(8,128)S(1)} collective-permute-done((f32[64,8]{0,1:T(8,128)S(1)}, f32[64,8]{0,1:T(8,128)S(1)}, u32[]{:S(2)}, u32[]{:S(2)}) %collective-permute-start.1) | collective-permute-done | bytes 2080 | tf_op jit(solution)/shard_map/while/body/eval_jaxpr/ppermute | solution.py:103
  130.2 3.3 while.109
  134.7 4.5 %collective-permute-done.1 = f32[64,8]{0,1:T(8,128)S(1)} collective-permute-done((f32[64,8]{0,1:T(8,128)S(1)}, f32[64,8]{0,1:T(8,128)S(1)}, u32[]{:S(2)}, u32[]{:S(2)}) %collective-permute-start.1) | collective-permute-done | bytes 2080 | tf_op jit(solution)/shard_map/while/body/eval_jaxpr/ppermute | solution.py:103
  139.3 3.3 while.109
  143.8 4.5 %collective-permute-done.1 = f32[64,8]{0,1:T(8,128)S(1)} collective-permute-done((f32[64,8]{0,1:T(8,128)S(1)}, f32[64,8]{0,1:T(8,128)S(1)}, u32[]{:S(2)}, u32[]{:S(2)}) %collective-permute-start.1) | collective-permute-done | bytes 2080 | tf_op jit(solution)/shard_map/while/body/eval_jaxpr/ppermute | solution.py:103
  151.8 29.5 %psum.28 = f32[64]{0:T(128)S(1)} all-reduce(f32[64]{0:T(128)S(1)} %fusion.51), channel_id=1, replica_groups=mesh['dp'=1,'seq'=8] {'seq'}, use_global_device_ids=true, to_apply=%region_12.13 | all-reduce | flops 64 | bytes 512 | tf_op jit(solution)/shard_map/psum | solution.py:108
  181.5 14.5 %convolution_bitcast_fusion = f32[640,4096]{1,0:T(8,128)} fusion(bf16[64,2,8,640]{3,2,1,0:T(8,128)(2,1)} %copy-done.4, f32[64,2,8,4096]{3,2,1,0:T(8,128)} %copy-done.2, f32[64,2,8]{2,1,0:T(2,128)S(1)} %get-tuple-element.851, f32[64,2,8]{2,1,0:T(2,128)S(1)} %get-tuple-element.850, f32[64,2,8]{2,1,0:T(2,128)S(1)} %get-tuple-element.849, ...), kind=kOutput, calls=%fused_computation.35 | convolution fusion | flops 5398069248 | bytes 30691328 | tf_op jit(solution)/shard_map/btuj,btuv->jv/dot_general | solution.py:71
  196.0 16.4 %fusion.57 = (bf16[64,2,640]{2,1,0:T(2,128)(2,1)S(1)}, bf16[64,2,8,640]{3,2,1,0:T(8,128)(2,1)}) fusion(bf16[64,2,8,640]{3,2,1,0:T(8,128)(2,1)} %copy-done.4, bf16[640,4096]{1,0:T(8,128)(2,1)} %param.24, f32[64,2,8,4096]{3,2,1,0:T(8,128)} %copy-done.2, f32[64,2,8]{2,1,0:T(2,128)S(1)} %get-tuple-element.851, f32[64,2,8]{2,1,0:T(2,128)S(1)} %get-tuple-element.850, ...), kind=kOutput, calls=%fused_computation.93 | convolution fusion | flops 5401919488 | bytes 26923008 | tf_op jit(solution)/shard_map/btuv,jv->btuj/dot_general | solution.py:65
  219.8 171.9 %all-reduce.9.cloned.1.call-done = (f32[640,640]{0,1:T(8,128)}, f32[640,640]{0,1:T(8,128)}, f32[640,4096]{1,0:T(8,128)}) async-done(((f32[640,640]{0,1:T(8,128)}, f32[640,640]{0,1:T(8,128)}, f32[640,4096]{1,0:T(8,128)}), (f32[640,640]{0,1:T(8,128)}, f32[640,640]{0,1:T(8,128)}, f32[640,4096]{1,0:T(8,128)})) %all-reduce.9.cloned.1.call-update) | async-done | bytes 13762576 | tf_op jit(solution)/shard_map/psum | solution.py:113
  397.2 9.4 %copy.162 = f32[640,4096]{1,0:T(8,128)} copy(f32[640,4096]{1,0:T(8,128)} %get-tuple-element.1320) | data formatting | bytes 20971520
  (311 shorter events, 75.3 us)
Async XLA Ops:
  7.2 2.0 copy-start
  7.2 384.6 %all-reduce.9.cloned.1.call-start = ((), (), s32[]{:S(2)}) async-start(), calls=%async_computation | async-start | bytes 27525120 | tf_op jit(solution)/shard_map/psum | solution.py:113
  7.2 4.7 %copy-start.10 = (bf16[640,4096]{1,0:T(8,128)(2,1)S(1)}, bf16[640,4096]{1,0:T(8,128)(2,1)}, u32[]{:S(2)}) copy-start(bf16[640,4096]{1,0:T(8,128)(2,1)} %param.24) | copy-start | bytes 15728644
  11.9 27.5 %copy-start.4 = (bf16[64,2,8,640]{3,2,1,0:T(8,128)(2,1)}, bf16[64,2,8,640]{3,2,1,0:T(8,128)(2,1)S(1)}, u32[]{:S(2)}) copy-start(bf16[64,2,8,640]{3,2,1,0:T(8,128)(2,1)S(1)} %tanh_convert_fusion) | copy-start | bytes 3932164
  18.9 5.7 %copy-start.2 = (f32[64,2,8,4096]{3,2,1,0:T(8,128)}, f32[64,2,8,4096]{3,2,1,0:T(8,128)S(1)}, u32[]{:S(2)}) copy-start(f32[64,2,8,4096]{3,2,1,0:T(8,128)S(1)} %get-tuple-element.856) | copy-start | bytes 50331652
  24.7 8.2 %copy-start.8 = (s32[64,7]{0,1:T(8,128)S(1)}, s32[64,7]{0,1:T(8,128)}, u32[]{:S(2)}) copy-start(s32[64,7]{0,1:T(8,128)} %param.25) | copy-start | bytes 5380
  42.5 41.3 %copy-start.7 = (s32[64]{0:T(128)S(1)}, s32[64]{0:T(128)}, u32[]{:S(2)}) copy-start(s32[64]{0:T(128)} %param.27) | copy-start | bytes 772
  42.5 41.3 %copy-start.9 = (s32[64]{0:T(128)S(1)}, s32[64]{0:T(128)}, u32[]{:S(2)}) copy-start(s32[64]{0:T(128)} %param.26) | copy-start | bytes 772
  46.2 3.6 collective-permute-start
  50.3 5.2 %collective-permute-start = (f32[64,8]{0,1:T(8,128)S(1)}, f32[64,8]{0,1:T(8,128)S(1)}, u32[]{:S(2)}, u32[]{:S(2)}) collective-permute-start(f32[64,8]{0,1:T(8,128)S(1)} %get-tuple-element.1120), channel_id=1, source_target_pairs={{0,1},{1,2},{2,3},{3,4},{4,5},{5,6},{6,7}} | collective-permute-start | bytes 6152 | tf_op jit(solution)/shard_map/while/body/eval_jaxpr/ppermute | solution.py:95
  56.1 4.9 %collective-permute-start = (f32[64,8]{0,1:T(8,128)S(1)}, f32[64,8]{0,1:T(8,128)S(1)}, u32[]{:S(2)}, u32[]{:S(2)}) collective-permute-start(f32[64,8]{0,1:T(8,128)S(1)} %get-tuple-element.1120), channel_id=1, source_target_pairs={{0,1},{1,2},{2,3},{3,4},{4,5},{5,6},{6,7}} | collective-permute-start | bytes 6152 | tf_op jit(solution)/shard_map/while/body/eval_jaxpr/ppermute | solution.py:95
  61.6 4.9 %collective-permute-start = (f32[64,8]{0,1:T(8,128)S(1)}, f32[64,8]{0,1:T(8,128)S(1)}, u32[]{:S(2)}, u32[]{:S(2)}) collective-permute-start(f32[64,8]{0,1:T(8,128)S(1)} %get-tuple-element.1120), channel_id=1, source_target_pairs={{0,1},{1,2},{2,3},{3,4},{4,5},{5,6},{6,7}} | collective-permute-start | bytes 6152 | tf_op jit(solution)/shard_map/while/body/eval_jaxpr/ppermute | solution.py:95
  67.1 4.9 %collective-permute-start = (f32[64,8]{0,1:T(8,128)S(1)}, f32[64,8]{0,1:T(8,128)S(1)}, u32[]{:S(2)}, u32[]{:S(2)}) collective-permute-start(f32[64,8]{0,1:T(8,128)S(1)} %get-tuple-element.1120), channel_id=1, source_target_pairs={{0,1},{1,2},{2,3},{3,4},{4,5},{5,6},{6,7}} | collective-permute-start | bytes 6152 | tf_op jit(solution)/shard_map/while/body/eval_jaxpr/ppermute | solution.py:95
  72.6 4.9 %collective-permute-start = (f32[64,8]{0,1:T(8,128)S(1)}, f32[64,8]{0,1:T(8,128)S(1)}, u32[]{:S(2)}, u32[]{:S(2)}) collective-permute-start(f32[64,8]{0,1:T(8,128)S(1)} %get-tuple-element.1120), channel_id=1, source_target_pairs={{0,1},{1,2},{2,3},{3,4},{4,5},{5,6},{6,7}} | collective-permute-start | bytes 6152 | tf_op jit(solution)/shard_map/while/body/eval_jaxpr/ppermute | solution.py:95
  78.1 4.9 %collective-permute-start = (f32[64,8]{0,1:T(8,128)S(1)}, f32[64,8]{0,1:T(8,128)S(1)}, u32[]{:S(2)}, u32[]{:S(2)}) collective-permute-start(f32[64,8]{0,1:T(8,128)S(1)} %get-tuple-element.1120), channel_id=1, source_target_pairs={{0,1},{1,2},{2,3},{3,4},{4,5},{5,6},{6,7}} | collective-permute-start | bytes 6152 | tf_op jit(solution)/shard_map/while/body/eval_jaxpr/ppermute | solution.py:95
  87.2 5.5 %collective-permute-start.1 = (f32[64,8]{0,1:T(8,128)S(1)}, f32[64,8]{0,1:T(8,128)S(1)}, u32[]{:S(2)}, u32[]{:S(2)}) collective-permute-start(f32[64,8]{0,1:T(8,128)S(1)} %get-tuple-element.1100), channel_id=1, source_target_pairs={{1,0},{2,1},{3,2},{4,3},{5,4},{6,5},{7,6}} | collective-permute-start | bytes 6152 | tf_op jit(solution)/shard_map/while/body/eval_jaxpr/ppermute | solution.py:103
  96.0 6.4 %collective-permute-start.1 = (f32[64,8]{0,1:T(8,128)S(1)}, f32[64,8]{0,1:T(8,128)S(1)}, u32[]{:S(2)}, u32[]{:S(2)}) collective-permute-start(f32[64,8]{0,1:T(8,128)S(1)} %get-tuple-element.1100), channel_id=1, source_target_pairs={{1,0},{2,1},{3,2},{4,3},{5,4},{6,5},{7,6}} | collective-permute-start | bytes 6152 | tf_op jit(solution)/shard_map/while/body/eval_jaxpr/ppermute | solution.py:103
  105.7 5.7 %collective-permute-start.1 = (f32[64,8]{0,1:T(8,128)S(1)}, f32[64,8]{0,1:T(8,128)S(1)}, u32[]{:S(2)}, u32[]{:S(2)}) collective-permute-start(f32[64,8]{0,1:T(8,128)S(1)} %get-tuple-element.1100), channel_id=1, source_target_pairs={{1,0},{2,1},{3,2},{4,3},{5,4},{6,5},{7,6}} | collective-permute-start | bytes 6152 | tf_op jit(solution)/shard_map/while/body/eval_jaxpr/ppermute | solution.py:103
  114.6 6.4 %collective-permute-start.1 = (f32[64,8]{0,1:T(8,128)S(1)}, f32[64,8]{0,1:T(8,128)S(1)}, u32[]{:S(2)}, u32[]{:S(2)}) collective-permute-start(f32[64,8]{0,1:T(8,128)S(1)} %get-tuple-element.1100), channel_id=1, source_target_pairs={{1,0},{2,1},{3,2},{4,3},{5,4},{6,5},{7,6}} | collective-permute-start | bytes 6152 | tf_op jit(solution)/shard_map/while/body/eval_jaxpr/ppermute | solution.py:103
  124.3 5.8 %collective-permute-start.1 = (f32[64,8]{0,1:T(8,128)S(1)}, f32[64,8]{0,1:T(8,128)S(1)}, u32[]{:S(2)}, u32[]{:S(2)}) collective-permute-start(f32[64,8]{0,1:T(8,128)S(1)} %get-tuple-element.1100), channel_id=1, source_target_pairs={{1,0},{2,1},{3,2},{4,3},{5,4},{6,5},{7,6}} | collective-permute-start | bytes 6152 | tf_op jit(solution)/shard_map/while/body/eval_jaxpr/ppermute | solution.py:103
  133.4 5.8 %collective-permute-start.1 = (f32[64,8]{0,1:T(8,128)S(1)}, f32[64,8]{0,1:T(8,128)S(1)}, u32[]{:S(2)}, u32[]{:S(2)}) collective-permute-start(f32[64,8]{0,1:T(8,128)S(1)} %get-tuple-element.1100), channel_id=1, source_target_pairs={{1,0},{2,1},{3,2},{4,3},{5,4},{6,5},{7,6}} | collective-permute-start | bytes 6152 | tf_op jit(solution)/shard_map/while/body/eval_jaxpr/ppermute | solution.py:103
  142.5 5.8 %collective-permute-start.1 = (f32[64,8]{0,1:T(8,128)S(1)}, f32[64,8]{0,1:T(8,128)S(1)}, u32[]{:S(2)}, u32[]{:S(2)}) collective-permute-start(f32[64,8]{0,1:T(8,128)S(1)} %get-tuple-element.1100), channel_id=1, source_target_pairs={{1,0},{2,1},{3,2},{4,3},{5,4},{6,5},{7,6}} | collective-permute-start | bytes 6152 | tf_op jit(solution)/shard_map/while/body/eval_jaxpr/ppermute | solution.py:103
  196.0 18.0 %copy-start.5 = (bf16[64,8,640]{2,1,0:T(8,128)(2,1)S(1)}, bf16[64,8,640]{2,1,0:T(8,128)(2,1)}, u32[]{:S(2)}) copy-start(bf16[64,8,640]{2,1,0:T(8,128)(2,1)} %param.21) | copy-start | bytes 1966084
  214.0 1.9 copy-start.6
  217.5 1.1 copy-start.3
  397.2 9.4 %copy-start.1 = (bf16[640,640]{1,0:T(8,128)(2,1)S(1)}, bf16[640,640]{1,0:T(8,128)(2,1)}, u32[]{:S(2)}) copy-start(bf16[640,640]{1,0:T(8,128)(2,1)} %param.23) | copy-start | bytes 2457604
Sparse Core Ops, SparseCore 0:
  217.6 174.0 all-reduce.8
where the time goes:
time: 414 us; the launch traced here: 413 us
  waiting for transfers between devices  210 us (51%)
  matrix products  54.8 us (13%)
  starting transfers between devices  36.8 us (9%)
  local copies, waits for them, and re-layouts  34.9 us (8%)
  other arithmetic  31.7 us (8%)
  blocking collectives  29.5 us (7%)
  between operations  14.4 us (3%)
    psum x1, waiting for transfers between devices, local_fn(): gw_enc, gw_pred, gw_out = lax.psum((gw_enc, gw_pred, gw_out), 'seq')  172 us
    ppermute x7, waiting for transfers between devices, beta_hop(): received = lax.ppermute(first_row, 'seq', bwd_pairs)  32.3 us
    psum x1, blocking collectives, local_fn(): log_prob = lax.psum(jnp.where(seq_idx == 0, first_row[:, 0], 0.0), 'seq')  29.5 us
    ppermute x7, starting transfers between devices, alpha_hop(): received = lax.ppermute(x_out, 'seq', fwd_pairs)  27.8 us
    unnamed x31, local copies, waits for them, and re-layouts  22.4 us
    dot_general x1, matrix products, joint_backward(): jnp.einsum('btuv,jv->btuj', d_logits, w_out, preferred_element_type=jnp.f...  16.4 us
    dot_general x1, matrix products, joint_backward(): jnp.einsum('btuj,btuv->jv', hidden, d_logits, preferred_element_type=jnp....  14.5 us
    ge x16, other arithmetic, frame_step(): beta_row = jnp.where((frame_id >= frame_len)[:, None], boundary, beta_row)  11 us
  transfers between devices with their start and end apart: 15, of which 15 were waited for; matrix products, arithmetic and copies ran while one was open for 0% of the time, Pallas kernels for 0%

commit v1 on v0

v1 whole, which is shorter than its diff:
```python
import jax
import jax.numpy as jnp
from jax import lax
from jax.experimental import pallas as pl
from jax.experimental.pallas import tpu as pltpu
from jax.sharding import PartitionSpec as P

NEG = -1.0e30
F32 = jnp.float32
BF16 = jnp.bfloat16
N_DEV = 8
DIM = 640
VOCAB = 4096
LANES = 1024
CHUNK = 256
VMEM_LIMIT = 66_000_000


def dot_nn(lhs, rhs):
    return lax.dot_general(lhs, rhs, (((1,), (0,)), ((), ())), preferred_element_type=F32)


def dot_nt(lhs, rhs):
    return lax.dot_general(lhs, rhs, (((1,), (1,)), ((), ())), preferred_element_type=F32)


def iota(shape, axis):
    return lax.broadcasted_iota(jnp.int32, shape, axis)


def eye(size):
    return jnp.where(iota((size, size), 0) == iota((size, size), 1), 1.0, 0.0).astype(BF16)


def transpose_into(dst, src, ident):
    cols = src.shape[1]
    for lo in range(0, cols, 256):
        width = min(256, cols - lo)
        dst[lo:lo + width, :] = dot_nt(ident[:width, :width], src[:, lo:lo + width]).astype(BF16)


def logaddexp(a, b):
    top = jnp.maximum(a, b)
    return top + jnp.log(1.0 + jnp.exp(-jnp.abs(a - b)))


class Peers:
    def __init__(self):
        self.dp = lax.axis_index('dp')
        self.me = lax.axis_index('seq')
        core = lax.rem(self.me, 2)
        col = lax.rem(self.me // 2, 2)
        row = self.me // 4
        self.pp = row * 4 + col * 2 + (1 - core)
        self.px = row * 4 + (1 - col) * 2 + core
        self.py = (1 - row) * 4 + col * 2 + core
        self.pd = (1 - row) * 4 + (1 - col) * 2 + core
        self.px_p = row * 4 + (1 - col) * 2 + (1 - core)
        self.py_p = (1 - row) * 4 + col * 2 + (1 - core)
        self.pd_p = (1 - row) * 4 + (1 - col) * 2 + (1 - core)

    def target(self, seq):
        return (self.dp, seq)


def remote(src, dst, send_sem, recv_sem, device):
    return pltpu.make_async_remote_copy(src_ref=src, dst_ref=dst, send_sem=send_sem, recv_sem=recv_sem,
                                        device_id=device, device_id_type=pl.DeviceIdType.MESH)


class Relay:
    def __init__(self, peers, view, half, send_sem, recv_sem):
        self.p = peers
        self.view = view
        self.half = half
        self.ssem = send_sem
        self.rsem = recv_sem

    def copy(self, kind, block, device):
        return remote(block, block, self.ssem.at[kind], self.rsem.at[kind], self.p.target(device))

    def start(self):
        p = self.p
        for kind, dev in ((1, p.px), (2, p.py), (0, p.pp)):
            self.copy(kind, self.view(p.me), dev).start()

    def pass_on(self):
        p = self.p
        self.copy(1, self.view(p.px), p.px).wait_recv()
        self.copy(4, self.half(p.px, 0), p.py).start()
        self.copy(3, self.view(p.px), p.pp).start()
        self.copy(2, self.view(p.py), p.py).wait_recv()
        self.copy(6, self.half(p.py, 1), p.px).start()
        self.copy(5, self.view(p.py), p.pp).start()

    def pass_diagonal(self):
        p = self.p
        self.copy(4, self.half(p.pd, 0), p.py).wait_recv()
        self.copy(7, self.half(p.pd, 0), p.pp).start()
        self.copy(6, self.half(p.pd, 1), p.px).wait_recv()
        self.copy(8, self.half(p.pd, 1), p.pp).start()

    def finish(self):
        p = self.p
        self.copy(0, self.view(p.pp), p.pp).wait_recv()
        self.copy(3, self.view(p.px_p), p.pp).wait_recv()
        self.copy(5, self.view(p.py_p), p.pp).wait_recv()
        self.copy(7, self.half(p.pd_p, 0), p.pp).wait_recv()
        self.copy(8, self.half(p.pd_p, 1), p.pp).wait_recv()
        self.copy(0, self.view(p.me), p.pp).wait_send()
        self.copy(1, self.view(p.me), p.px).wait_send()
        self.copy(2, self.view(p.me), p.py).wait_send()
        self.copy(3, self.view(p.px), p.pp).wait_send()
        self.copy(4, self.half(p.px, 0), p.py).wait_send()
        self.copy(5, self.view(p.py), p.pp).wait_send()
        self.copy(6, self.half(p.py, 1), p.px).wait_send()
        self.copy(7, self.half(p.pd, 0), p.pp).wait_send()
        self.copy(8, self.half(p.pd, 1), p.pp).wait_send()


class Direct:
    def __init__(self, peers, src, dst, send_sem, recv_sem):
        self.p = peers
        self.src = src
        self.dst = dst
        self.ssem = send_sem
        self.rsem = recv_sem

    def copy(self, k, to, source):
        return remote(self.src(to), self.dst(source), self.ssem.at[k], self.rsem.at[k], self.p.target(to))

    def start(self):
        for k in range(1, N_DEV):
            self.copy(k, lax.rem(self.p.me + k, N_DEV), self.p.me).start()

    def wait_recv(self):
        for k in range(1, N_DEV):
            self.copy(k, lax.rem(self.p.me + k, N_DEV), lax.rem(self.p.me + N_DEV - k, N_DEV)).wait_recv()

    def wait_send(self):
        for k in range(1, N_DEV):
            self.copy(k, lax.rem(self.p.me + k, N_DEV), self.p.me).wait_send()


def pick_rows(ref, offsets, group):
    out = None
    for u, off in enumerate(offsets):
        part = ref[off:off + 24, :]
        out = part if out is None else jnp.where(group == u, part, out)
    return out


def lattice(lse, z_blank, z_lab, aux, me, skew, stats):
    lane = iota((1, 128), 1)
    group = lax.rem(lane // 8, 8)
    n_frames = aux[1, pl.ds(me, 1), :]
    n_labels = aux[2, pl.ds(me, 1), :]

    def by_time(x):
        return jnp.concatenate([x, pltpu.roll(x, 64, 1)], axis=0)

    skew[...] = jnp.zeros_like(skew)
    skew[0, 8:24, :] = by_time(z_blank - lse)
    skew[1, 8:24, :] = by_time(z_lab - lse)
    offsets = [8 - u for u in range(8)]
    group24 = jnp.broadcast_to(group, (24, 128))
    blank = pick_rows(skew.at[0], offsets, group24)
    lab = pick_rows(skew.at[1], offsets, group24)

    first_u = group == 0
    last_u = group == 7
    alpha = jnp.where(first_u, 0.0, NEG).astype(F32)
    alphas = [alpha]
    for d in range(1, 23):
        stay = alpha + blank[d - 1:d]
        step = jnp.where(first_u, NEG, pltpu.roll(alpha + lab[d - 1:d], 8, 1))
        alpha = logaddexp(stay, step)
        alphas.append(alpha)
    alphas.append(jnp.full((1, 128), NEG, F32))
    bound = jnp.where(group == n_labels, 0.0, NEG).astype(F32)
    beta = bound
    nexts, ups = [None] * 24, [None] * 24
    nexts[23] = ups[23] = jnp.full((1, 128), NEG, F32)
    for d in range(22, -1, -1):
        up = jnp.where(last_u, NEG, pltpu.roll(beta, 120, 1))
        nexts[d], ups[d] = beta, up
        new = logaddexp(beta + blank[d:d + 1], up + lab[d:d + 1])
        beta = jnp.where(d - group >= n_frames, bound, new)
    log_p = jnp.where(lane < 8, beta, 0.0)
    for shift in (8, 16, 32, 64):
        log_p = log_p + pltpu.roll(log_p, shift, 1)

    alphas = jnp.concatenate(alphas, axis=0)
    nexts = jnp.concatenate(nexts, axis=0)
    ups = jnp.concatenate(ups, axis=0)
    frame = iota((24, 128), 0) - group24
    ok = (frame >= 0) & (frame < n_frames)
    occ_b = jnp.where(ok, jnp.exp(jnp.minimum(alphas + blank + nexts - log_p, 0.0)), 0.0)
    occ_l = jnp.where(ok & (group24 < 7), jnp.exp(jnp.minimum(alphas + lab + ups - log_p, 0.0)), 0.0)
    skew[0, 0:24, :] = occ_b
    skew[1, 0:24, :] = occ_l
    offsets = list(range(8))
    low = jnp.broadcast_to(lane < 64, (8, 128))

    def by_tile(x):
        return jnp.where(low, x[0:8], pltpu.roll(x[8:16], 64, 1))

    stats[me, 0:8, :] = lse
    stats[me, 8:16, :] = by_tile(pick_rows(skew.at[0], offsets, group24))
    stats[me, 16:24, :] = by_tile(pick_rows(skew.at[1], offsets, group24))
    stats[me, 24:32, :] = jnp.broadcast_to(log_p, (8, 128))


def grad_logits(z, stats, block, lab, first_id, col0=0, has_blank=None):
    rows, cols = z.shape
    ids = iota((rows, 128), 0) + first_id
    tiles = []
    for k in range(cols // 128):
        kk = k + col0
        lse = stats[block, kk:kk + 1, :]
        occ_b = stats[block, 8 + kk:9 + kk, :]
        occ_l = stats[block, 16 + kk:17 + kk, :]
        tile = jnp.exp(z[:, k * 128:(k + 1) * 128] - lse) * (occ_b + occ_l)
        tile = tile - jnp.where(ids == lab, occ_l, 0.0)
        head = tile[0:16] - jnp.where(ids[0:16] == 0, occ_b, 0.0)
        tiles.append(jnp.concatenate([head, tile[16:]], axis=0).astype(BF16))
    return jnp.concatenate(tiles, axis=1)


def main_kernel(enc, g, w_enc, w_pred, w_out, aux,
                gw_buf, da_all, dc_all, f_all, stats,
                wt, ht, sel, act, wet, wpt, dh, skew, a2a_s, a2a_r, f_s, f_r, st_s, st_r,
                gw_s, gw_r, da_s, da_r, dc_s, dc_r):
    p = Peers()
    me = p.me
    barrier = pltpu.get_barrier_semaphore()
    for k in range(1, N_DEV):
        pl.semaphore_signal(barrier, inc=1, device_id=p.target(lax.rem(me + k, N_DEV)),
                            device_id_type=pl.DeviceIdType.MESH)
    pl.semaphore_wait(barrier, N_DEV - 1)

    def rows16(i):
        return pl.ds(pl.multiple_of(i * 16, 16), 16)

    copies = []
    for k in range(1, N_DEV):
        to = lax.rem(me + k, N_DEV)
        copies.append(remote(enc.at[rows16(to), :], f_all.at[to, rows16(me), :], a2a_s.at[k], a2a_r.at[k], p.target(to)))
    for c in copies:
        c.start()
    f_all[me, rows16(me), :] = enc[rows16(me), :]

    ident = eye(256)
    transpose_into(wet, w_enc, ident)
    transpose_into(wpt, w_pred, ident)

    def transpose_out(c, _):
        lo = pl.multiple_of(c * CHUNK, CHUNK)
        wt[pl.ds(lo, CHUNK), :] = dot_nt(ident, w_out[:, pl.ds(lo, CHUNK)]).astype(BF16)
        return 0

    lax.fori_loop(0, VOCAB // CHUNK, transpose_out, 0)
    row = iota((192, LANES), 0)
    col = iota((192, LANES), 1)
    t_id = col // 128 + 8 * (lax.rem(col, 128) // 64)
    u_id = lax.rem(col // 8, 8)
    b_id = lax.rem(col, 8)
    a_row = 2 * (row // 16) + lax.rem(row, 2)
    a_b = lax.rem(row // 2, 8)
    c_row = row - 128
    hit = jnp.where(row < 128, jnp.where((a_row == t_id) & (a_b == b_id), 1.0, 0.0),
                    jnp.where((c_row // 8 == b_id) & (lax.rem(c_row, 8) == u_id), 1.0, 0.0))
    sel[...] = hit.astype(BF16)

    for d in range(N_DEV):
        act[d, :, 128:192] = dot_nt(wpt[...], g[d * 64:(d + 1) * 64, :]).astype(BF16)

    for k in range(1, N_DEV):
        src = lax.rem(me + N_DEV - k, N_DEV)
        remote(enc.at[rows16(me), :], f_all.at[me, rows16(src), :], a2a_s.at[k], a2a_r.at[k], p.target(src)).wait_recv()

    f_gather = Direct(p, lambda d: f_all.at[me], lambda i: f_all.at[i], f_s, f_r)
    f_gather.start()

    def hidden(d):
        act[d, :, 0:128] = dot_nt(wet[...], f_all[d]).astype(BF16)
        ht[d] = jnp.tanh(dot_nn(act[d], sel[...])).astype(BF16)

    hidden(me)
    lab_own = aux[0, pl.ds(me, 1), :]

    def tile8(x):
        return jnp.concatenate([x] * 8, axis=1)

    lab_row = tile8(lab_own)

    def forward(c, carry):
        top, total, z_lab = carry
        lo = pl.multiple_of(c * CHUNK, CHUNK)
        z = dot_nn(wt[pl.ds(lo, CHUNK), :], ht[me]).reshape(CHUNK // 8, 8, LANES)
        new = jnp.maximum(top, jnp.max(z, axis=0))
        total = total * jnp.exp(top - new) + jnp.sum(jnp.exp(z - new[None]), axis=0)
        ids = iota((CHUNK // 8, 8, LANES), 0) * 8 + iota((CHUNK // 8, 8, LANES), 1) + lo
        z_lab = z_lab + jnp.sum(jnp.where(ids == lab_row[None], z, 0.0), axis=0)
        return new, total, z_lab

    start = (jnp.full((8, LANES), NEG, F32), jnp.zeros((8, LANES), F32), jnp.zeros((8, LANES), F32))
    top, total, z_lab = lax.fori_loop(0, VOCAB // CHUNK, forward, start)
    peak = jnp.max(top, axis=0, keepdims=True)
    lse = peak + jnp.log(jnp.sum(total * jnp.exp(top - peak), axis=0, keepdims=True))
    z_lab = jnp.sum(z_lab, axis=0, keepdims=True)
    z_blank = dot_nn(wt[0:16, :], ht[me])[0:1]

    def tiles(x):
        return jnp.concatenate([x[:, k * 128:(k + 1) * 128] for k in range(8)], axis=0)

    lattice(tiles(lse), tiles(z_blank), tiles(z_lab), aux, me, skew, stats)
    st_gather = Direct(p, lambda d: stats.at[me], lambda i: stats.at[i], st_s, st_r)
    st_gather.start()

    f_gather.wait_recv()

    def hidden_other(k, _):
        hidden(lax.rem(me + k, N_DEV))
        return 0

    lax.fori_loop(1, N_DEV, hidden_other, 0)
    st_gather.wait_recv()

    relays = []
    for c in range(2):
        def view(e, c=c):
            return gw_buf.at[2 * e + c]

        def half(e, h, c=c):
            return gw_buf.at[2 * e + c, pl.ds(h * 320, 320), :]

        relay = Relay(p, view, half, gw_s.at[c], gw_r.at[c])
        relays.append(relay)
        first = pl.multiple_of(me * 512 + c * CHUNK, CHUNK)
        gw_buf[2 * me + c] = jnp.zeros((DIM, CHUNK), F32)

        def block(d, _, c=c, first=first):
            z = dot_nn(wt[pl.ds(first, CHUNK), :], ht[d])
            dz = grad_logits(z, stats, d, aux[0, pl.ds(d, 1), :], first)
            gw_buf[2 * me + c] += dot_nt(ht[d], dz)
            return 0

        lax.fori_loop(0, N_DEV, block, 0)
        relay.start()

    dh[...] = jnp.zeros_like(dh)

    def backward(c, _):
        lo = pl.multiple_of(c * 512, 512)
        z = dot_nn(wt[pl.ds(lo, 512), :], ht[me])
        dz = grad_logits(z, stats, me, lab_own, lo)
        dh[...] += dot_nn(w_out[:, pl.ds(lo, 512)], dz)
        return 0

    lax.fori_loop(0, VOCAB // 512, backward, 0)
    relays[0].pass_on()
    h32 = ht[me].astype(F32)
    dp = (dh[...] * (1.0 - h32 * h32)).astype(BF16)
    sums = dot_nt(dp, sel[...])
    da_all[me] = sums[:, 0:128].astype(BF16)
    dc_all[me] = jnp.concatenate([sums[0:320, 128:192], sums[320:640, 128:192]], axis=1)
    da_relay = Relay(p, lambda e: da_all.at[e], lambda e, h: da_all.at[e, pl.ds(h * 320, 320), :], da_s, da_r)
    dc_relay = Relay(p, lambda e: dc_all.at[e], lambda e, h: dc_all.at[e, pl.ds(h * 160, 160), :], dc_s, dc_r)
    da_relay.start()
    dc_relay.start()
    relays[1].pass_on()
    da_relay.pass_on()
    dc_relay.pass_on()
    for relay in (relays[0], relays[1], da_relay, dc_relay):
        relay.pass_diagonal()
    for relay in (relays[0], relays[1], da_relay, dc_relay):
        relay.finish()
    for c in copies:
        c.wait_send()
    f_gather.wait_send()
    st_gather.wait_send()


def final_kernel(gw_buf, da_all, dc_all, f_all, g, w_enc, gw_out, grad_enc, gw_enc, gw_pred, ft, gt, out_sem):
    me = lax.axis_index('seq')
    flush = []
    for n in range(VOCAB // CHUNK):
        flush.append(pltpu.make_async_copy(gw_buf.at[n], gw_out.at[:, n * CHUNK:(n + 1) * CHUNK], out_sem.at[n]))
        flush[-1].start()
    ident = eye(256)
    for d in range(N_DEV):
        for lo in range(0, DIM, 256):
            width = min(256, DIM - lo)
            ft[lo:lo + width, d * 128:(d + 1) * 128] = dot_nt(ident[:width, :width], f_all[d, :, lo:lo + width]).astype(BF16)
    transpose_into(gt, g, ident)
    da = jnp.concatenate([da_all[d] for d in range(N_DEV)], axis=1)
    gw_enc[...] = dot_nt(ft[...], da)
    pick = jnp.where(iota((16, 128), 1) == iota((16, 128), 0) + me * 16, 1.0, 0.0).astype(BF16)
    mine = jnp.concatenate([dot_nt(pick, da_all[d]).astype(BF16) for d in range(N_DEV)], axis=0)
    grad_enc[...] = dot_nt(mine, w_enc[...]).astype(BF16)
    dc = jnp.concatenate([jnp.concatenate([dc_all[d, :, 0:64], dc_all[d, :, 64:128]], axis=0) for d in range(N_DEV)], axis=1)
    gw_pred[...] = dot_nt(gt[...], dc.astype(BF16))
    for copy in flush:
        copy.wait()


def vmem():
    return pl.BlockSpec(memory_space=pltpu.VMEM)


def solution(mesh):
    dma = pltpu.SemaphoreType.DMA

    def local_fn(enc_out, pred_out, w_enc, w_pred, w_out, labels, frame_len, label_len):
        n_utt = pred_out.shape[0]
        enc = enc_out.reshape(2 * n_utt, DIM)
        g = pred_out.reshape(8 * n_utt, DIM)
        lab = jnp.concatenate([labels, jnp.full((n_utt, 1), -1, jnp.int32)], axis=1)
        lab = lab.reshape(8, 8, 8).transpose(0, 2, 1)
        lens = jnp.broadcast_to(jnp.stack([frame_len, label_len]).reshape(2, 8, 1, 8), (2, 8, 8, 8))
        aux = jnp.concatenate([lab[None], lens], axis=0).reshape(3, 8, 64)
        aux = jnp.concatenate([aux, aux], axis=2)
        gw_buf, da_all, dc_all, f_all, stats = pl.pallas_call(
            main_kernel,
            out_shape=(jax.ShapeDtypeStruct((16, DIM, CHUNK), F32),
                       jax.ShapeDtypeStruct((8, DIM, 128), BF16),
                       jax.ShapeDtypeStruct((8, DIM // 2, 128), F32),
                       jax.ShapeDtypeStruct((8, 128, DIM), BF16),
                       jax.ShapeDtypeStruct((8, 32, 128), F32)),
            in_specs=[vmem()] * 6,
            out_specs=(vmem(),) * 5,
            scratch_shapes=[pltpu.VMEM((VOCAB, DIM), BF16), pltpu.VMEM((8, DIM, LANES), BF16),
                            pltpu.VMEM((192, LANES), BF16), pltpu.VMEM((8, DIM, 192), BF16),
                            pltpu.VMEM((DIM, DIM), BF16), pltpu.VMEM((DIM, DIM), BF16),
                            pltpu.VMEM((DIM, LANES), F32), pltpu.VMEM((2, 40, 128), F32),
                            dma((8,)), dma((8,)), dma((8,)), dma((8,)), dma((8,)), dma((8,)),
                            dma((2, 9)), dma((2, 9)), dma((9,)), dma((9,)), dma((9,)), dma((9,))],
            compiler_params=pltpu.CompilerParams(collective_id=0, has_side_effects=True, vmem_limit_bytes=VMEM_LIMIT),
        )(enc, g, w_enc, w_pred, w_out, aux)
        gw_out, grad_enc, gw_enc, gw_pred = pl.pallas_call(
            final_kernel,
            out_shape=(jax.ShapeDtypeStruct((DIM, VOCAB), F32),
                       jax.ShapeDtypeStruct((2 * n_utt, DIM), BF16),
                       jax.ShapeDtypeStruct((DIM, DIM), F32),
                       jax.ShapeDtypeStruct((DIM, DIM), F32)),
            in_specs=[vmem()] * 6,
            out_specs=(pl.BlockSpec(memory_space=pl.ANY), vmem(), vmem(), vmem()),
            scratch_shapes=[pltpu.VMEM((DIM, LANES), BF16), pltpu.VMEM((DIM, 512), BF16), dma((16,))],
            compiler_params=pltpu.CompilerParams(vmem_limit_bytes=VMEM_LIMIT),
        )(gw_buf, da_all, dc_all, f_all, g, w_enc)
        loss = -stats[:, 24, 0:8].reshape(n_utt)
        return loss, grad_enc.reshape(enc_out.shape), gw_enc, gw_pred, gw_out

    in_specs = (P('dp', 'seq', None), P('dp', None, None), P(None, None), P(None, None), P(None, None), P('dp', None), P('dp'), P('dp'))
    out_specs = (P('dp'), P('dp', 'seq', None), P('dp', None), P('dp', None), P('dp', None))
    return jax.shard_map(local_fn, mesh=mesh, in_specs=in_specs, out_specs=out_specs, check_vma=False)
```

time: 414 us -> 130 us (0.31)
  waiting for transfers between devices: 210 us -> 0 us
  Pallas kernels: 0 us -> 122 us
  matrix products: 54.8 us -> 0 us
  starting transfers between devices: 36.8 us -> 0 us
  other arithmetic: 31.7 us -> 1.46 us
  blocking collectives: 29.5 us -> 0 us
  local copies, waits for them, and re-layouts: 34.9 us -> 6.28 us
  between operations: 14.4 us -> 0.67 us
    psum x1 -> x0, waiting for transfers between devices: 172 us -> none  [local_fn(): gw_enc, gw_pred, gw_out = lax.psum((gw_enc, gw_pred, gw_out), 'seq')]
    pallas_call x0 -> x2, Pallas kernels: none -> 122 us  [the longest x1 109 us: local_fn(): pl.pallas_call(main_kernel, out_shape=(jax.ShapeDtypeStruct((16, DIM, CHU...]
    dot_general x10 -> x0, matrix products: 54.8 us -> none  [the longest x1 16.4 us: joint_backward(): jnp.einsum('btuv,jv->btuj', d_logits, w_out, preferred_element_type=jnp.f...]
    ppermute x14 -> x0, waiting for transfers between devices: 37.9 us -> none  [the longest x7 32.3 us: beta_hop(): received = lax.ppermute(first_row, 'seq', bwd_pairs)]
    ppermute x14 -> x0, starting transfers between devices: 36.8 us -> none  [the longest x7 27.8 us: alpha_hop(): received = lax.ppermute(x_out, 'seq', fwd_pairs)]
    psum x1 -> x0, blocking collectives: 29.5 us -> none  [local_fn(): log_prob = lax.psum(jnp.where(seq_idx == 0, first_row[:, 0], 0.0), 'seq')]
    unnamed x31 -> x0, local copies, waits for them, and re-layouts: 22.4 us -> none
    ge x16 -> x0, other arithmetic: 11 us -> none  [frame_step(): beta_row = jnp.where((frame_id >= frame_len)[:, None], boundary, beta_row)]
  transfers between devices with their start and end apart: 15 -> 0, of which waited for: 15 -> 0; matrix products, arithmetic and copies ran while one was open for 0% -> 0% of each run, Pallas kernels for 0% -> 0%
where the time goes in v1:
time: 130 us
  Pallas kernels  122 us (94%)
  local copies, waits for them, and re-layouts  6.28 us (5%)
  other arithmetic  1.46 us (1%)
    pallas_call x1, Pallas kernels, local_fn(): pl.pallas_call(main_kernel, out_shape=(jax.ShapeDtypeStruct((16, DIM, CHU...  109 us
    pallas_call x1, Pallas kernels, local_fn(): pl.pallas_call(final_kernel, out_shape=(jax.ShapeDtypeStruct((DIM, VOCAB)...  12.2 us

profile of v1, /device:TPU:0, one launch (start us, length us, event | category | flops | bytes accessed | tf_op | source)
XLA Modules:
  0.0 130.0 jit_solution(6403921316654137879)
XLA Ops:
  0.6 0.7 concatenate.15
  1.3 0.7 stack.9
  2.1 0.7 stack.10
  2.8 0.1 reshape.34
  2.9 0.1 concatenate.16
  3.0 0.1 concatenate.17
  3.1 0.7 add_add_fusion.aux
  3.7 1.6 %reshape.32.enc = bf16[128,640]{1,0:T(8,128)(2,1)} reshape(bf16[64,2,640]{2,1,0:T(2,128)(2,1)} %param.8) | data formatting | bytes 327680 | tf_op jit(solution)/shard_map/reshape | solution.py:417
  5.4 109.4 %shard_map.119 = (f32[16,640,256]{2,1,0:T(8,128)}, bf16[8,640,128]{2,1,0:T(8,128)(2,1)}, f32[8,320,128]{2,1,0:T(8,128)}, bf16[8,128,640]{2,1,0:T(8,128)(2,1)}, f32[8,32,128]{2,1,0:T(8,128)}) custom-call(bf16[128,640]{1,0:T(8,128)(2,1)} %reshape.32.enc, bf16[512,640]{1,0:T(8,128)(2,1)} %bitcast.10, bf16[640,640]{1,0:T(8,128)(2,1)} %w_enc.3, ...), custom_call_target="tpu_custom_call" | custom-call | tf_op jit(solution)/shard_map/pallas_call | solution.py:424
  114.7 0.8 negate_reduce_fusion
  115.5 0.6 neg.7
  116.1 12.2 %shard_map.120 = (f32[640,4096]{1,0:T(8,128)}, bf16[128,640]{1,0:T(8,128)(2,1)}, f32[640,640]{1,0:T(8,128)}, f32[640,640]{1,0:T(8,128)}) custom-call(f32[16,640,256]{2,1,0:T(8,128)} %get-tuple-element.15.gw_buf, bf16[8,640,128]{2,1,0:T(8,128)(2,1)} %get-tuple-element.16.da_all, f32[8,320,128]{2,1,0:T(8,128)} %get-tuple-element.17.dc_all, ...), custom_call_target="tpu_custom_call" | custom-call | tf_op jit(solution)/shard_map/pallas_call | solution.py:441
  128.3 1.6 %reshape.35 = bf16[64,2,640]{2,1,0:T(2,128)(2,1)} reshape(bf16[128,640]{1,0:T(8,128)(2,1)} %get-tuple-element.19) | data formatting | bytes 327680 | tf_op jit(solution)/shard_map/reshape | solution.py:453
  (3 shorter events, 0.0 us)

commit v2 on v1

--- a/solution.py
+++ b/solution.py
@@ -13,7 +13,8 @@
 VOCAB = 4096
 LANES = 1024
 CHUNK = 256
-VMEM_LIMIT = 66_000_000
+MAIN_VMEM = 48 << 20
+LAST_VMEM = 20 << 20
 
 
 def dot_nn(lhs, rhs):
@@ -51,6 +52,8 @@
         core = lax.rem(self.me, 2)
         col = lax.rem(self.me // 2, 2)
         row = self.me // 4
+        self.core = core
+        self.diag = lax.rem(row + col, 2)
         self.pp = row * 4 + col * 2 + (1 - core)
         self.px = row * 4 + (1 - col) * 2 + core
         self.py = (1 - row) * 4 + col * 2 + core
@@ -118,6 +121,49 @@
         self.copy(8, self.half(p.pd, 1), p.pp).wait_send()
 
 
+class Pair:
+    def __init__(self, peers, buf, mine, other, send_sem, recv_sem):
+        self.p = peers
+        self.buf = buf
+        self.mine = mine
+        self.other = other
+        self.ssem = send_sem
+        self.rsem = recv_sem
+
+    def copy(self, c, kind, block, device):
+        return remote(block, block, self.ssem.at[c, kind], self.rsem.at[c, kind], self.p.target(device))
+
+    def half(self, base, core, c, h):
+        return self.buf.at[(base + core) * 4 + c, h * 320:(h + 1) * 320, :]
+
+    def start(self, c):
+        p = self.p
+        self.copy(c, 1, self.half(self.mine, p.core, c, 0), p.px).start()
+        self.copy(c, 2, self.half(self.mine, p.core, c, 1), p.py).start()
+        self.copy(c, 0, self.buf.at[(self.mine + p.core) * 4 + c], p.pp).start()
+
+    def pass_on(self, c):
+        p = self.p
+        low = self.half(self.other, p.core, c, 0)
+        high = self.half(self.other, p.core, c, 1)
+        self.copy(c, 1, low, p.px).wait_recv()
+        self.copy(c, 3, low, p.pp).start()
+        self.copy(c, 2, high, p.py).wait_recv()
+        self.copy(c, 4, high, p.pp).start()
+
+    def finish(self, c):
+        p = self.p
+        twin = 1 - p.core
+        self.copy(c, 0, self.buf.at[(self.mine + twin) * 4 + c], p.pp).wait_recv()
+        self.copy(c, 3, self.half(self.other, twin, c, 0), p.pp).wait_recv()
+        self.copy(c, 4, self.half(self.other, twin, c, 1), p.pp).wait_recv()
+        self.copy(c, 0, self.buf.at[(self.mine + p.core) * 4 + c], p.pp).wait_send()
+        self.copy(c, 1, self.half(self.mine, p.core, c, 0), p.px).wait_send()
+        self.copy(c, 2, self.half(self.mine, p.core, c, 1), p.py).wait_send()
+        self.copy(c, 3, self.half(self.other, p.core, c, 0), p.pp).wait_send()
+        self.copy(c, 4, self.half(self.other, p.core, c, 1), p.pp).wait_send()
+
+
 class Direct:
     def __init__(self, peers, src, dst, send_sem, recv_sem):
         self.p = peers
@@ -150,11 +196,9 @@
     return out
 
 
-def lattice(lse, z_blank, z_lab, aux, me, skew, stats):
+def lattice(lse, z_blank, z_lab, n_frames, n_labels, me, skew, stats):
     lane = iota((1, 128), 1)
     group = lax.rem(lane // 8, 8)
-    n_frames = aux[1, pl.ds(me, 1), :]
-    n_labels = aux[2, pl.ds(me, 1), :]
 
     def by_time(x):
         return jnp.concatenate([x, pltpu.roll(x, 64, 1)], axis=0)
@@ -227,16 +271,43 @@
     return jnp.concatenate(tiles, axis=1)
 
 
-def main_kernel(enc, g, w_enc, w_pred, w_out, aux,
+def own_lengths(ref, scratch, me):
+    scratch[...] = jnp.zeros_like(scratch)
+    scratch[:, 0:64] = ref[...]
+    x = pltpu.roll(scratch[...], lax.rem(128 - 8 * me, 128), 1)
+    x = jnp.where(iota((1, 128), 1) < 8, x, 0)
+    for shift in (8, 16, 32, 64):
+        x = x + pltpu.roll(x, shift, 1)
+    return x
+
+
+def spread_labels(labels, scratch, lab):
+    scratch[...] = jnp.full_like(scratch, -1)
+    scratch[0:7, 0:64] = labels[...]
+    scratch[0:7, 64:128] = labels[...]
+    x = pltpu.roll(scratch[...], 0, 1, stride=8, stride_axis=0)
+    keep = lax.rem(iota((8, 128), 1) // 8, 8) == iota((8, 128), 0)
+    for d in range(N_DEV):
+        turned = pltpu.roll(x, 128 - 8 * d, 1) if d else x
+        lab[d:d + 1, :] = jnp.sum(jnp.where(keep, turned, 0), axis=0, keepdims=True)
+
+
+def main_kernel(enc3, g, w_enc, w_pred, w_hbm, labels, frame_len, label_len,
                 gw_buf, da_all, dc_all, f_all, stats,
-                wt, ht, sel, act, wet, wpt, dh, skew, a2a_s, a2a_r, f_s, f_r, st_s, st_r,
-                gw_s, gw_r, da_s, da_r, dc_s, dc_r):
+                enc, w_out, wt, ht, sel, act, wet, wpt, dh, dzs, skew, lab, lab_x, len_x, load_sem,
+                a2a_s, a2a_r, f_s, f_r, st_s, st_r, gw_s, gw_r, da_s, da_r, dc_s, dc_r):
     p = Peers()
     me = p.me
     barrier = pltpu.get_barrier_semaphore()
     for k in range(1, N_DEV):
         pl.semaphore_signal(barrier, inc=1, device_id=p.target(lax.rem(me + k, N_DEV)),
                             device_id_type=pl.DeviceIdType.MESH)
+    loads = []
+    for k in range(4):
+        cols = slice(k * 1024, (k + 1) * 1024)
+        loads.append(pltpu.make_async_copy(w_hbm.at[:, cols], w_out.at[:, cols], load_sem.at[k]))
+        loads[-1].start()
+    enc[...] = enc3[...].reshape(128, DIM)
     pl.semaphore_wait(barrier, N_DEV - 1)
 
     def rows16(i):
@@ -253,13 +324,6 @@
     ident = eye(256)
     transpose_into(wet, w_enc, ident)
     transpose_into(wpt, w_pred, ident)
-
-    def transpose_out(c, _):
-        lo = pl.multiple_of(c * CHUNK, CHUNK)
-        wt[pl.ds(lo, CHUNK), :] = dot_nt(ident, w_out[:, pl.ds(lo, CHUNK)]).astype(BF16)
-        return 0
-
-    lax.fori_loop(0, VOCAB // CHUNK, transpose_out, 0)
     row = iota((192, LANES), 0)
     col = iota((192, LANES), 1)
     t_id = col // 128 + 8 * (lax.rem(col, 128) // 64)
@@ -271,9 +335,20 @@
     hit = jnp.where(row < 128, jnp.where((a_row == t_id) & (a_b == b_id), 1.0, 0.0),
                     jnp.where((c_row // 8 == b_id) & (lax.rem(c_row, 8) == u_id), 1.0, 0.0))
     sel[...] = hit.astype(BF16)
-
+    spread_labels(labels, lab_x, lab)
+    n_frames = own_lengths(frame_len, len_x, me)
+    n_labels = own_lengths(label_len, len_x, me)
     for d in range(N_DEV):
         act[d, :, 128:192] = dot_nt(wpt[...], g[d * 64:(d + 1) * 64, :]).astype(BF16)
+
+    def transpose_out(c, _):
+        lo = pl.multiple_of(c * CHUNK, CHUNK)
+        wt[pl.ds(lo, CHUNK), :] = dot_nt(ident, w_out[:, pl.ds(lo, CHUNK)]).astype(BF16)
+        return 0
+
+    for k in range(4):
+        loads[k].wait()
+        lax.fori_loop(4 * k, 4 * k + 4, transpose_out, 0, unroll=4)
 
     for k in range(1, N_DEV):
         src = lax.rem(me + N_DEV - k, N_DEV)
@@ -287,12 +362,8 @@
         ht[d] = jnp.tanh(dot_nn(act[d], sel[...])).astype(BF16)
 
     hidden(me)
-    lab_own = aux[0, pl.ds(me, 1), :]
-
-    def tile8(x):
-        return jnp.concatenate([x] * 8, axis=1)
-
-    lab_row = tile8(lab_own)
+    lab_own = lab[pl.ds(me, 1), :]
+    lab_row = jnp.concatenate([lab_own] * 8, axis=1)
 
     def forward(c, carry):
         top, total, z_lab = carry
@@ -305,7 +376,7 @@
         return new, total, z_lab
 
     start = (jnp.full((8, LANES), NEG, F32), jnp.zeros((8, LANES), F32), jnp.zeros((8, LANES), F32))
-    top, total, z_lab = lax.fori_loop(0, VOCAB // CHUNK, forward, start)
+    top, total, z_lab = lax.fori_loop(0, VOCAB // CHUNK, forward, start, unroll=4)
     peak = jnp.max(top, axis=0, keepdims=True)
     lse = peak + jnp.log(jnp.sum(total * jnp.exp(top - peak), axis=0, keepdims=True))
     z_lab = jnp.sum(z_lab, axis=0, keepdims=True)
@@ -314,7 +385,7 @@
     def tiles(x):
         return jnp.concatenate([x[:, k * 128:(k + 1) * 128] for k in range(8)], axis=0)
 
-    lattice(tiles(lse), tiles(z_blank), tiles(z_lab), aux, me, skew, stats)
+    lattice(tiles(lse), tiles(z_blank), tiles(z_lab), n_frames, n_labels, me, skew, stats)
     st_gather = Direct(p, lambda d: stats.at[me], lambda i: stats.at[i], st_s, st_r)
     st_gather.start()
 
@@ -324,42 +395,40 @@
         hidden(lax.rem(me + k, N_DEV))
         return 0
 
-    lax.fori_loop(1, N_DEV, hidden_other, 0)
+    lax.fori_loop(1, N_DEV, hidden_other, 0, unroll=7)
     st_gather.wait_recv()
 
-    relays = []
-    for c in range(2):
-        def view(e, c=c):
-            return gw_buf.at[2 * e + c]
-
-        def half(e, h, c=c):
-            return gw_buf.at[2 * e + c, pl.ds(h * 320, 320), :]
-
-        relay = Relay(p, view, half, gw_s.at[c], gw_r.at[c])
-        relays.append(relay)
-        first = pl.multiple_of(me * 512 + c * CHUNK, CHUNK)
-        gw_buf[2 * me + c] = jnp.zeros((DIM, CHUNK), F32)
-
-        def block(d, _, c=c, first=first):
-            z = dot_nn(wt[pl.ds(first, CHUNK), :], ht[d])
-            dz = grad_logits(z, stats, d, aux[0, pl.ds(d, 1), :], first)
-            gw_buf[2 * me + c] += dot_nt(ht[d], dz)
-            return 0
-
-        lax.fori_loop(0, N_DEV, block, 0)
-        relay.start()
-
+    mine = 2 * p.diag
+    pair = Pair(p, gw_buf, mine, 2 - mine, gw_s, gw_r)
+    own_set = mine + p.core
     dh[...] = jnp.zeros_like(dh)
 
-    def backward(c, _):
-        lo = pl.multiple_of(c * 512, 512)
+    def chunk(c, _):
+        n = own_set * 4 + c
+        first = pl.multiple_of(n * CHUNK, CHUNK)
+        rows = wt[pl.ds(first, CHUNK), :]
+        z = dot_nn(rows, ht[0])
+        for d in range(N_DEV):
+            z_next = dot_nn(rows, ht[d + 1]) if d + 1 < N_DEV else None
+            dz = grad_logits(z, stats, d, lab[d:d + 1, :], first)
+            dzs[d] = dz
+            part = dot_nt(ht[d], dz)
+            gw_buf[n] = part if d == 0 else gw_buf[n] + part
+            z = z_next
+        pair.start(c)
+        dh[...] += dot_nn(w_out[:, pl.ds(first, CHUNK)], dzs[me])
+        return 0
+
+    lax.fori_loop(0, 4, chunk, 0)
+
+    def backward(i, _):
+        lo = pl.multiple_of(lax.rem(2 * own_set + 2 + i, 8) * 512, 512)
         z = dot_nn(wt[pl.ds(lo, 512), :], ht[me])
         dz = grad_logits(z, stats, me, lab_own, lo)
         dh[...] += dot_nn(w_out[:, pl.ds(lo, 512)], dz)
         return 0
 
-    lax.fori_loop(0, VOCAB // 512, backward, 0)
-    relays[0].pass_on()
+    lax.fori_loop(0, 6, backward, 0, unroll=2)
     h32 = ht[me].astype(F32)
     dp = (dh[...] * (1.0 - h32 * h32)).astype(BF16)
     sums = dot_nt(dp, sel[...])
@@ -369,20 +438,23 @@
     dc_relay = Relay(p, lambda e: dc_all.at[e], lambda e, h: dc_all.at[e, pl.ds(h * 160, 160), :], dc_s, dc_r)
     da_relay.start()
     dc_relay.start()
-    relays[1].pass_on()
+    for c in range(4):
+        pair.pass_on(c)
     da_relay.pass_on()
     dc_relay.pass_on()
-    for relay in (relays[0], relays[1], da_relay, dc_relay):
-        relay.pass_diagonal()
-    for relay in (relays[0], relays[1], da_relay, dc_relay):
-        relay.finish()
+    da_relay.pass_diagonal()
+    dc_relay.pass_diagonal()
+    for c in range(4):
+        pair.finish(c)
+    da_relay.finish()
+    dc_relay.finish()
     for c in copies:
         c.wait_send()
     f_gather.wait_send()
     st_gather.wait_send()
 
 
-def final_kernel(gw_buf, da_all, dc_all, f_all, g, w_enc, gw_out, grad_enc, gw_enc, gw_pred, ft, gt, out_sem):
+def final_kernel(gw_buf, da_all, dc_all, f_all, stats, g, w_enc, loss, grad_enc, gw_enc, gw_pred, gw_out, ft, gt, out_sem):
     me = lax.axis_index('seq')
     flush = []
     for n in range(VOCAB // CHUNK):
@@ -398,7 +470,12 @@
     gw_enc[...] = dot_nt(ft[...], da)
     pick = jnp.where(iota((16, 128), 1) == iota((16, 128), 0) + me * 16, 1.0, 0.0).astype(BF16)
     mine = jnp.concatenate([dot_nt(pick, da_all[d]).astype(BF16) for d in range(N_DEV)], axis=0)
-    grad_enc[...] = dot_nt(mine, w_enc[...]).astype(BF16)
+    grad_enc[...] = dot_nt(mine, w_enc[...]).reshape(64, 2, DIM).astype(BF16)
+    total = jnp.zeros((1, 128), F32)
+    for d in range(N_DEV):
+        own = jnp.where(iota((1, 128), 1) < 8, stats[d, 24:25, :], 0.0)
+        total = total - (pltpu.roll(own, 8 * d, 1) if d else own)
+    loss[...] = total[:, 0:64]
     dc = jnp.concatenate([jnp.concatenate([dc_all[d, :, 0:64], dc_all[d, :, 64:128]], axis=0) for d in range(N_DEV)], axis=1)
     gw_pred[...] = dot_nt(gt[...], dc.astype(BF16))
     for copy in flush:
@@ -414,43 +491,39 @@
 
     def local_fn(enc_out, pred_out, w_enc, w_pred, w_out, labels, frame_len, label_len):
         n_utt = pred_out.shape[0]
-        enc = enc_out.reshape(2 * n_utt, DIM)
         g = pred_out.reshape(8 * n_utt, DIM)
-        lab = jnp.concatenate([labels, jnp.full((n_utt, 1), -1, jnp.int32)], axis=1)
-        lab = lab.reshape(8, 8, 8).transpose(0, 2, 1)
-        lens = jnp.broadcast_to(jnp.stack([frame_len, label_len]).reshape(2, 8, 1, 8), (2, 8, 8, 8))
-        aux = jnp.concatenate([lab[None], lens], axis=0).reshape(3, 8, 64)
-        aux = jnp.concatenate([aux, aux], axis=2)
-        gw_buf, da_all, dc_all, f_all, stats = pl.pallas_call(
+        hbm = pl.BlockSpec(memory_space=pl.ANY)
+        handed = pl.pallas_call(
             main_kernel,
-            out_shape=(jax.ShapeDtypeStruct((16, DIM, CHUNK), F32),
-                       jax.ShapeDtypeStruct((8, DIM, 128), BF16),
-                       jax.ShapeDtypeStruct((8, DIM // 2, 128), F32),
-                       jax.ShapeDtypeStruct((8, 128, DIM), BF16),
-                       jax.ShapeDtypeStruct((8, 32, 128), F32)),
-            in_specs=[vmem()] * 6,
+            out_shape=(pltpu.VMEM((16, DIM, CHUNK), F32), pltpu.VMEM((8, DIM, 128), BF16),
+                       pltpu.VMEM((8, DIM // 2, 128), F32), pltpu.VMEM((8, 128, DIM), BF16),
+                       pltpu.VMEM((8, 32, 128), F32)),
+            in_specs=[vmem()] * 4 + [hbm] + [vmem()] * 3,
             out_specs=(vmem(),) * 5,
-            scratch_shapes=[pltpu.VMEM((VOCAB, DIM), BF16), pltpu.VMEM((8, DIM, LANES), BF16),
+            scratch_shapes=[pltpu.VMEM((128, DIM), BF16), pltpu.VMEM((DIM, VOCAB), BF16),
+                            pltpu.VMEM((VOCAB, DIM), BF16), pltpu.VMEM((8, DIM, LANES), BF16),
                             pltpu.VMEM((192, LANES), BF16), pltpu.VMEM((8, DIM, 192), BF16),
                             pltpu.VMEM((DIM, DIM), BF16), pltpu.VMEM((DIM, DIM), BF16),
-                            pltpu.VMEM((DIM, LANES), F32), pltpu.VMEM((2, 40, 128), F32),
+                            pltpu.VMEM((DIM, LANES), F32), pltpu.VMEM((8, CHUNK, LANES), BF16),
+                            pltpu.VMEM((2, 40, 128), F32), pltpu.VMEM((8, 128), jnp.int32),
+                            pltpu.VMEM((8, 128), jnp.int32), pltpu.VMEM((1, 128), jnp.int32), dma((4,)),
                             dma((8,)), dma((8,)), dma((8,)), dma((8,)), dma((8,)), dma((8,)),
-                            dma((2, 9)), dma((2, 9)), dma((9,)), dma((9,)), dma((9,)), dma((9,))],
-            compiler_params=pltpu.CompilerParams(collective_id=0, has_side_effects=True, vmem_limit_bytes=VMEM_LIMIT),
-        )(enc, g, w_enc, w_pred, w_out, aux)
-        gw_out, grad_enc, gw_enc, gw_pred = pl.pallas_call(
+                            dma((4, 5)), dma((4, 5)), dma((9,)), dma((9,)), dma((9,)), dma((9,))],
+            compiler_params=pltpu.CompilerParams(collective_id=0, has_side_effects=True, vmem_limit_bytes=MAIN_VMEM),
+        )(enc_out, g, w_enc, w_pred, w_out, labels.T, frame_len.reshape(1, n_utt), label_len.reshape(1, n_utt))
+        loss, grad_enc, gw_enc, gw_pred, gw_out = pl.pallas_call(
             final_kernel,
-            out_shape=(jax.ShapeDtypeStruct((DIM, VOCAB), F32),
-                       jax.ShapeDtypeStruct((2 * n_utt, DIM), BF16),
+            out_shape=(jax.ShapeDtypeStruct((1, n_utt), F32),
+                       jax.ShapeDtypeStruct(enc_out.shape, BF16),
                        jax.ShapeDtypeStruct((DIM, DIM), F32),
-                       jax.ShapeDtypeStruct((DIM, DIM), F32)),
-            in_specs=[vmem()] * 6,
-            out_specs=(pl.BlockSpec(memory_space=pl.ANY), vmem(), vmem(), vmem()),
+                       jax.ShapeDtypeStruct((DIM, DIM), F32),
+                       jax.ShapeDtypeStruct((DIM, VOCAB), F32)),
+            in_specs=[vmem()] * 7,
+            out_specs=(vmem(), vmem(), vmem(), vmem(), hbm),
             scratch_shapes=[pltpu.VMEM((DIM, LANES), BF16), pltpu.VMEM((DIM, 512), BF16), dma((16,))],
-            compiler_params=pltpu.CompilerParams(vmem_limit_bytes=VMEM_LIMIT),
-        )(gw_buf, da_all, dc_all, f_all, g, w_enc)
-        loss = -stats[:, 24, 0:8].reshape(n_utt)
-        return loss, grad_enc.reshape(enc_out.shape), gw_enc, gw_pred, gw_out
+            compiler_params=pltpu.CompilerParams(vmem_limit_bytes=LAST_VMEM),
+        )(*handed, g, w_enc)
+        return loss.reshape(n_utt), grad_enc, gw_enc, gw_pred, gw_out
 
     in_specs = (P('dp', 'seq', None), P('dp', None, None), P(None, None), P(None, None), P(None, None), P('dp', None), P('dp'), P('dp'))
     out_specs = (P('dp'), P('dp', 'seq', None), P('dp', None), P('dp', None), P('dp', None))

time: 130 us -> 96.5 us (0.74)
  Pallas kernels: 122 us -> 95.5 us
  local copies, waits for them, and re-layouts: 6.28 us -> 0.01 us
  other arithmetic: 1.46 us -> 0 us
    pallas_call x2, Pallas kernels: 122 us -> 95.5 us  [the longest x1 86.4 us: local_fn(): pl.pallas_call(main_kernel, out_shape=(pltpu.VMEM((16, DIM, CHUNK), F32),...]
    reshape x4 -> x0, local copies, waits for them, and re-layouts: 3.37 us -> none  [the longest x1 1.65 us: local_fn(): return (loss, grad_enc.reshape(enc_out.shape), gw_enc, gw_pred, gw_out)]
    another operation x2 -> x0, local copies, waits for them, and re-layouts: 1.47 us -> none  [local_fn(): jnp.stack([frame_len, label_len]).reshape(2, 8, 1, 8)]
where the time goes in v2:
time: 96.5 us; the launch traced here: 96.4 us
  Pallas kernels  95.5 us (99%)
    pallas_call x1, Pallas kernels, local_fn(): pl.pallas_call(main_kernel, out_shape=(pltpu.VMEM((16, DIM, CHUNK), F32),...  86.4 us
    pallas_call x1, Pallas kernels, local_fn(): pl.pallas_call(final_kernel, out_shape=(jax.ShapeDtypeStruct((1, n_utt),...  9.06 us

profile of v2, /device:TPU:0, one launch (start us, length us, event | category | flops | bytes accessed | tf_op | source)
XLA Modules:
  0.0 96.4 jit_solution(17515690268909850442)
XLA Ops:
  0.6 0.0 copy-start
  0.6 0.0 copy-start.1
  0.7 86.4 %shard_map.119 = (f32[16,640,256]{2,1,0:T(8,128)S(1)}, bf16[8,640,128]{2,1,0:T(8,128)(2,1)S(1)}, f32[8,320,128]{2,1,0:T(8,128)S(1)}, bf16[8,128,640]{2,1,0:T(8,128)(2,1)S(1)}, f32[8,32,128]{2,1,0:T(8,128)S(1)}) custom-call(bf16[64,2,640]{2,1,0:T(2,128)(2,1)} %enc3.1, bf16[512,640]{1,0:T(8,128)(2,1)} %bitcast.5, bf16[640,640]{1,0:T(8,128)(2,1)} %w_enc.3, ...), custom_call_target="tpu_custom_call" | custom-call | tf_op jit(solution)/shard_map/pallas_call | solution.py:496
  87.1 0.0 copy-done
  87.1 0.0 copy-done.1
  87.1 9.1 %shard_map.120 = (f32[1,64]{1,0:T(1,128)}, bf16[64,2,640]{2,1,0:T(2,128)(2,1)}, f32[640,640]{1,0:T(8,128)}, f32[640,640]{1,0:T(8,128)}, f32[640,4096]{1,0:T(8,128)}) custom-call(f32[16,640,256]{2,1,0:T(8,128)S(1)} %get-tuple-element.15.gw_buf, bf16[8,640,128]{2,1,0:T(8,128)(2,1)S(1)} %get-tuple-element.16.da_all, ...), custom_call_target="tpu_custom_call" | custom-call | tf_op jit(solution)/shard_map/pallas_call | solution.py:514
Async XLA Ops:
  0.6 86.5 %copy-start = (bf16[640,640]{1,0:T(8,128)(2,1)S(1)}, bf16[640,640]{1,0:T(8,128)(2,1)}, u32[]{:S(2)}) copy-start(bf16[640,640]{1,0:T(8,128)(2,1)} %w_enc.3) | copy-start | bytes 2457604
  0.6 86.5 %copy-start.1 = (bf16[64,8,640]{2,1,0:T(8,128)(2,1)S(1)}, bf16[64,8,640]{2,1,0:T(8,128)(2,1)}, u32[]{:S(2)}) copy-start(bf16[64,8,640]{2,1,0:T(8,128)(2,1)} %param.9) | copy-start | bytes 1966084

commit v3 on v2

v3 whole, which is shorter than its diff:
```python
import jax
import jax.numpy as jnp
from jax import lax
from jax.experimental import pallas as pl
from jax.experimental.pallas import tpu as pltpu
from jax.sharding import PartitionSpec as P

NEG = -1.0e30
F32 = jnp.float32
BF16 = jnp.bfloat16
N_DEV = 8
DIM = 640
VOCAB = 4096
LANES = 1024
CHUNK = 256
MAIN_VMEM = 52_600_000
LAST_VMEM = 1_000_000
OCT, DIAGS, HALF, TILE, WIDE, MID = 8, 24, 64, 128, 192, 320


def dot_nn(lhs, rhs):
    return lax.dot_general(lhs, rhs, (((1,), (0,)), ((), ())), preferred_element_type=F32)


def dot_nt(lhs, rhs):
    return lax.dot_general(lhs, rhs, (((1,), (1,)), ((), ())), preferred_element_type=F32)


def iota(shape, axis):
    return lax.broadcasted_iota(jnp.int32, shape, axis)


def eye(size):
    return jnp.where(iota((size, size), 0) == iota((size, size), 1), 1.0, 0.0).astype(BF16)


def transpose_into(dst, src, ident):
    cols = src.shape[1]
    for lo in range(0, cols, CHUNK):
        width = min(CHUNK, cols - lo)
        dst[lo:lo + width, :] = dot_nt(ident[:width, :width], src[:, lo:lo + width]).astype(BF16)


def logaddexp(a, b):
    top = jnp.maximum(a, b)
    return top + jnp.log(1.0 + jnp.exp(-jnp.abs(a - b)))


class Peers:
    def __init__(self):
        self.dp = lax.axis_index('dp')
        self.me = lax.axis_index('seq')
        core = lax.rem(self.me, 2)
        col = lax.rem(self.me // 2, 2)
        row = self.me // 4
        self.core = core
        self.diag = lax.rem(row + col, 2)
        self.pp = row * 4 + col * 2 + (1 - core)
        self.px = row * 4 + (1 - col) * 2 + core
        self.py = (1 - row) * 4 + col * 2 + core
        self.pd = (1 - row) * 4 + (1 - col) * 2 + core
        self.px_p = row * 4 + (1 - col) * 2 + (1 - core)
        self.py_p = (1 - row) * 4 + col * 2 + (1 - core)
        self.pd_p = (1 - row) * 4 + (1 - col) * 2 + (1 - core)

    def target(self, seq):
        return (self.dp, seq)


def remote(src, dst, send_sem, recv_sem, device):
    return pltpu.make_async_remote_copy(src_ref=src, dst_ref=dst, send_sem=send_sem, recv_sem=recv_sem,
                                        device_id=device, device_id_type=pl.DeviceIdType.MESH)


class Relay:
    def __init__(self, peers, view, half, send_sem, recv_sem):
        self.p = peers
        self.view = view
        self.half = half
        self.ssem = send_sem
        self.rsem = recv_sem

    def copy(self, kind, block, device):
        return remote(block, block, self.ssem.at[kind], self.rsem.at[kind], self.p.target(device))

    def stage(self, number, x, y, d):
        p = self.p
        if number == 0:
            base, pairs = 0, ((p.px, self.view(p.me)), (p.py, self.view(p.me)), (p.pp, self.view(x)))
        elif number == 1:
            base, pairs = 3, ((p.py, self.half(x, 0)), (p.px, self.half(y, 1)), (p.pp, self.view(x)), (p.pp, self.view(y)))
        else:
            base, pairs = 7, ((p.pp, self.half(d, 0)), (p.pp, self.half(d, 1)))
        return [self.copy(base + i, block, device) for i, (device, block) in enumerate(pairs)]

    def start(self):
        for copy in self.stage(0, self.p.me, None, None):
            copy.start()

    def pass_on(self):
        p = self.p
        from_x = self.copy(0, self.view(p.px), p.px)
        from_y = self.copy(1, self.view(p.py), p.py)
        to_y, to_x, x_over, y_over = self.stage(1, p.px, p.py, None)
        from_x.wait_recv()
        to_y.start()
        x_over.start()
        from_y.wait_recv()
        to_x.start()
        y_over.start()

    def pass_diagonal(self):
        p = self.p
        self.copy(3, self.half(p.pd, 0), p.py).wait_recv()
        self.copy(4, self.half(p.pd, 1), p.px).wait_recv()
        for copy in self.stage(2, None, None, p.pd):
            copy.start()

    def finish(self):
        p = self.p
        self.stage(0, p.pp, None, None)[2].wait_recv()
        for copy in self.stage(1, p.px_p, p.py_p, None)[2:] + self.stage(2, None, None, p.pd_p):
            copy.wait_recv()
        for copy in self.stage(0, p.me, None, None) + self.stage(1, p.px, p.py, None) + self.stage(2, None, None, p.pd):
            copy.wait_send()


class Pair:
    def __init__(self, peers, buf, mine, other, send_sem, recv_sem):
        self.p = peers
        self.buf = buf
        self.mine = mine
        self.other = other
        self.ssem = send_sem
        self.rsem = recv_sem

    def copy(self, c, kind, block, device):
        return remote(block, block, self.ssem.at[c, kind], self.rsem.at[c, kind], self.p.target(device))

    def half(self, base, core, c, h):
        return self.buf.at[(base + core) * 4 + c, h * MID:(h + 1) * MID, :]

    def start(self, c):
        p = self.p
        self.copy(c, 1, self.half(self.mine, p.core, c, 0), p.px).start()
        self.copy(c, 2, self.half(self.mine, p.core, c, 1), p.py).start()
        self.copy(c, 0, self.buf.at[(self.mine + p.core) * 4 + c], p.pp).start()

    def pass_on(self, c):
        p = self.p
        low = self.half(self.other, p.core, c, 0)
        high = self.half(self.other, p.core, c, 1)
        self.copy(c, 1, low, p.px).wait_recv()
        self.copy(c, 3, low, p.pp).start()
        self.copy(c, 2, high, p.py).wait_recv()
        self.copy(c, 4, high, p.pp).start()

    def finish(self, c):
        p = self.p
        twin = 1 - p.core
        self.copy(c, 0, self.buf.at[(self.mine + twin) * 4 + c], p.pp).wait_recv()
        self.copy(c, 3, self.half(self.other, twin, c, 0), p.pp).wait_recv()
        self.copy(c, 4, self.half(self.other, twin, c, 1), p.pp).wait_recv()
        self.copy(c, 0, self.buf.at[(self.mine + p.core) * 4 + c], p.pp).wait_send()
        self.copy(c, 1, self.half(self.mine, p.core, c, 0), p.px).wait_send()
        self.copy(c, 2, self.half(self.mine, p.core, c, 1), p.py).wait_send()
        self.copy(c, 3, self.half(self.other, p.core, c, 0), p.pp).wait_send()
        self.copy(c, 4, self.half(self.other, p.core, c, 1), p.pp).wait_send()


class Direct:
    def __init__(self, peers, src, dst, send_sem, recv_sem):
        self.p = peers
        self.src = src
        self.dst = dst
        self.ssem = send_sem
        self.rsem = recv_sem

    def copy(self, k, to, source):
        return remote(self.src(to), self.dst(source), self.ssem.at[k], self.rsem.at[k], self.p.target(to))

    def start(self):
        for k in range(1, N_DEV):
            self.copy(k, lax.rem(self.p.me + k, N_DEV), self.p.me).start()

    def wait_recv(self):
        for k in range(1, N_DEV):
            self.copy(k, lax.rem(self.p.me + k, N_DEV), lax.rem(self.p.me + N_DEV - k, N_DEV)).wait_recv()

    def wait_send(self):
        for k in range(1, N_DEV):
            self.copy(k, lax.rem(self.p.me + k, N_DEV), self.p.me).wait_send()


def pick_rows(ref, offsets, group):
    out = None
    for u, off in enumerate(offsets):
        part = ref[off:off + DIAGS, :]
        out = part if out is None else jnp.where(group == u, part, out)
    return out


def lattice(lse, z_blank, z_lab, n_frames, n_labels, me, skew, stats):
    lane = iota((1, TILE), 1)
    group = lax.rem(lane // OCT, OCT)

    def by_time(x):
        return jnp.concatenate([x, pltpu.roll(x, HALF, 1)], axis=0)

    skew[...] = jnp.zeros_like(skew)
    skew[0, OCT:DIAGS, :] = by_time(z_blank - lse)
    skew[1, OCT:DIAGS, :] = by_time(z_lab - lse)
    offsets = [OCT - u for u in range(OCT)]
    group24 = jnp.broadcast_to(group, (DIAGS, TILE))
    blank = pick_rows(skew.at[0], offsets, group24)
    lab = pick_rows(skew.at[1], offsets, group24)

    first_u = group == 0
    last_u = group == 7
    alpha = jnp.where(first_u, 0.0, NEG).astype(F32)
    alphas = [alpha]
    for d in range(1, 23):
        stay = alpha + blank[d - 1:d]
        step = jnp.where(first_u, NEG, pltpu.roll(alpha + lab[d - 1:d], OCT, 1))
        alpha = logaddexp(stay, step)
        alphas.append(alpha)
    alphas.append(jnp.full((1, TILE), NEG, F32))
    bound = jnp.where(group == n_labels, 0.0, NEG).astype(F32)
    beta = bound
    nexts, ups = [None] * DIAGS, [None] * DIAGS
    nexts[23] = ups[23] = jnp.full((1, TILE), NEG, F32)
    for d in range(22, -1, -1):
        up = jnp.where(last_u, NEG, pltpu.roll(beta, 120, 1))
        nexts[d], ups[d] = beta, up
        new = logaddexp(beta + blank[d:d + 1], up + lab[d:d + 1])
        beta = jnp.where(d - group >= n_frames, bound, new)
    log_p = jnp.where(lane < OCT, beta, 0.0)
    for shift in (OCT, 16, 32, HALF):
        log_p = log_p + pltpu.roll(log_p, shift, 1)

    alphas = jnp.concatenate(alphas, axis=0)
    nexts = jnp.concatenate(nexts, axis=0)
    ups = jnp.concatenate(ups, axis=0)
    frame = iota((DIAGS, TILE), 0) - group24
    ok = (frame >= 0) & (frame < n_frames)
    occ_b = jnp.where(ok, jnp.exp(jnp.minimum(alphas + blank + nexts - log_p, 0.0)), 0.0)
    occ_l = jnp.where(ok & (group24 < 7), jnp.exp(jnp.minimum(alphas + lab + ups - log_p, 0.0)), 0.0)
    skew[0, 0:DIAGS, :] = occ_b
    skew[1, 0:DIAGS, :] = occ_l
    offsets = list(range(OCT))
    low = jnp.broadcast_to(lane < HALF, (OCT, TILE))

    def by_tile(x):
        return jnp.where(low, x[0:OCT], pltpu.roll(x[OCT:16], HALF, 1))

    stats[me, 0:OCT, :] = lse
    stats[me, OCT:16, :] = by_tile(pick_rows(skew.at[0], offsets, group24))
    stats[me, 16:DIAGS, :] = by_tile(pick_rows(skew.at[1], offsets, group24))
    stats[me, DIAGS:32, :] = jnp.broadcast_to(log_p, (OCT, TILE))


def grad_logits(z, stats, block, lab, first_id, col0=0, has_blank=None):
    rows, cols = z.shape
    ids = iota((rows, TILE), 0) + first_id
    tiles = []
    for k in range(cols // TILE):
        kk = k + col0
        lse = stats[block, kk:kk + 1, :]
        occ_b = stats[block, OCT + kk:9 + kk, :]
        occ_l = stats[block, 16 + kk:17 + kk, :]
        tile = jnp.exp(z[:, k * TILE:(k + 1) * TILE] - lse) * (occ_b + occ_l)
        tile = tile - jnp.where(ids == lab, occ_l, 0.0)
        head = tile[0:16] - jnp.where(ids[0:16] == 0, occ_b, 0.0)
        tiles.append(jnp.concatenate([head, tile[16:]], axis=0).astype(BF16))
    return jnp.concatenate(tiles, axis=1)


def own_lengths(ref, scratch, me):
    scratch[...] = jnp.zeros_like(scratch)
    scratch[:, 0:HALF] = ref[...]
    x = pltpu.roll(scratch[...], lax.rem(TILE - OCT * me, TILE), 1)
    x = jnp.where(iota((1, TILE), 1) < OCT, x, 0)
    for shift in (OCT, 16, 32, HALF):
        x = x + pltpu.roll(x, shift, 1)
    return x


def spread_labels(labels, scratch, lab):
    scratch[...] = jnp.full_like(scratch, -1)
    scratch[0:7, 0:HALF] = labels[...]
    scratch[0:7, HALF:TILE] = labels[...]
    x = pltpu.roll(scratch[...], 0, 1, stride=OCT, stride_axis=0)
    keep = lax.rem(iota((OCT, TILE), 1) // OCT, OCT) == iota((OCT, TILE), 0)
    for d in range(N_DEV):
        turned = pltpu.roll(x, TILE - OCT * d, 1) if d else x
        lab[d:d + 1, :] = jnp.sum(jnp.where(keep, turned, 0), axis=0, keepdims=True)


def main_kernel(enc3, g_hbm, we_hbm, wp_hbm, w_hbm, labels, frame_len, label_len,
                loss, grad_enc, gw_enc, gw_pred, gw_buf,
                enc, g, w_enc, w_out, wt, ht, zs, sel, act, c_all, wet, da_all, dc_all, f_all, stats, skew, lab, lab_x, len_x,
                load_sem, a2a_s, a2a_r, st_s, st_r, gw_s, gw_r, f_s, f_r, da_s, da_r, dc_s, dc_r):
    p = Peers()
    me = p.me
    barrier = pltpu.get_barrier_semaphore()
    for k in range(1, N_DEV):
        pl.semaphore_signal(barrier, inc=1, device_id=p.target(lax.rem(me + k, N_DEV)),
                            device_id_type=pl.DeviceIdType.MESH)
    w_pred, wpt = ht.at[0, :, 0:DIM], ht.at[1, :, 0:DIM]
    loads = [(wp_hbm, w_pred), (g_hbm, g), (we_hbm, w_enc)]
    for lo in range(0, VOCAB, LANES):
        loads.append((w_hbm.at[:, lo:lo + LANES], w_out.at[:, lo:lo + LANES]))
    loads = [pltpu.make_async_copy(src, dst, load_sem.at[k]) for k, (src, dst) in enumerate(loads)]
    for copy in loads:
        copy.start()
    enc[...] = enc3[...].reshape(TILE, DIM)
    pl.semaphore_wait(barrier, N_DEV - 1)

    def rows16(i):
        return pl.ds(pl.multiple_of(i * 16, 16), 16)

    copies = []
    for k in range(1, N_DEV):
        to = lax.rem(me + k, N_DEV)
        copies.append(remote(enc.at[rows16(to), :], f_all.at[to, rows16(me), :], a2a_s.at[k], a2a_r.at[k], p.target(to)))
    for copy in copies:
        copy.start()
    f_all[me, rows16(me), :] = enc[rows16(me), :]

    ident = eye(CHUNK)
    row = iota((WIDE, LANES), 0)
    col = iota((WIDE, LANES), 1)
    t_id = col // TILE + OCT * (lax.rem(col, TILE) // HALF)
    u_id = lax.rem(col // OCT, OCT)
    b_id = lax.rem(col, OCT)
    a_row = 2 * (row // 16) + lax.rem(row, 2)
    a_b = lax.rem(row // 2, OCT)
    c_row = row - TILE
    hit = jnp.where(row < TILE, jnp.where((a_row == t_id) & (a_b == b_id), 1.0, 0.0),
                    jnp.where((c_row // OCT == b_id) & (lax.rem(c_row, OCT) == u_id), 1.0, 0.0))
    sel[...] = hit.astype(BF16)
    spread_labels(labels, lab_x, lab)
    n_frames = own_lengths(frame_len, len_x, me)
    n_labels = own_lengths(label_len, len_x, me)
    first_loads, last_loads = loads[:3], loads[3:]
    for copy in first_loads:
        copy.wait()
    transpose_into(wpt, w_pred, ident)
    transpose_into(wet, w_enc, ident)
    c_cols = dot_nt(wpt[...], g[...]).astype(BF16)
    for d in range(N_DEV):
        c_all[d] = c_cols[:, d * HALF:(d + 1) * HALF]

    def transpose_out(c, _):
        lo = pl.multiple_of(c * CHUNK, CHUNK)
        wt[pl.ds(lo, CHUNK), :] = dot_nt(ident, w_out[:, pl.ds(lo, CHUNK)]).astype(BF16)
        return 0

    for k, copy in enumerate(last_loads):
        copy.wait()
        lax.fori_loop(4 * k, 4 * k + 4, transpose_out, 0, unroll=4)

    for k in range(1, N_DEV):
        src = lax.rem(me + N_DEV - k, N_DEV)
        remote(enc.at[rows16(me), :], f_all.at[me, rows16(src), :], a2a_s.at[k], a2a_r.at[k], p.target(src)).wait_recv()

    f_relay = Relay(p, lambda e: f_all.at[e], lambda e, h: f_all.at[e, h * HALF:(h + 1) * HALF, :], f_s, f_r)
    f_relay.start()

    def hidden(d, slot):
        act[slot, :, 0:TILE] = dot_nt(wet[...], f_all[d]).astype(BF16)
        act[slot, :, TILE:WIDE] = c_all[d]
        ht[d] = jnp.tanh(dot_nn(act[slot], sel[...])).astype(BF16)

    hidden(me, 0)
    lab_own = lab[pl.ds(me, 1), :]
    lab_row = jnp.concatenate([lab_own] * OCT, axis=1)

    def forward(c, carry):
        top, total, z_lab = carry
        lo = pl.multiple_of(c * CHUNK, CHUNK)
        z = dot_nn(wt[pl.ds(lo, CHUNK), :], ht[me])
        zs[pl.ds(lo, CHUNK), :] = z
        z = z.reshape(CHUNK // OCT, OCT, LANES)
        new = jnp.maximum(top, jnp.max(z, axis=0))
        total = total * jnp.exp(top - new) + jnp.sum(jnp.exp(z - new[None]), axis=0)
        ids = iota(z.shape, 0) * OCT + iota(z.shape, 1) + lo
        z_lab = z_lab + jnp.sum(jnp.where(ids == lab_row[None], z, 0.0), axis=0)
        return new, total, z_lab

    carry = (jnp.full((OCT, LANES), NEG, F32), jnp.zeros((OCT, LANES), F32), jnp.zeros((OCT, LANES), F32))
    carry = lax.fori_loop(0, OCT, forward, carry, unroll=4)
    f_relay.pass_on()
    top, total, z_lab = lax.fori_loop(OCT, 16, forward, carry, unroll=4)
    f_relay.pass_diagonal()
    peak = jnp.max(top, axis=0, keepdims=True)
    lse = peak + jnp.log(jnp.sum(total * jnp.exp(top - peak), axis=0, keepdims=True))
    z_lab = jnp.sum(z_lab, axis=0, keepdims=True)
    z_blank = zs[0:1, :]

    def tiles(x):
        return jnp.concatenate([x[:, k * TILE:(k + 1) * TILE] for k in range(OCT)], axis=0)

    lattice(tiles(lse), tiles(z_blank), tiles(z_lab), n_frames, n_labels, me, skew, stats)
    st_gather = Direct(p, lambda d: stats.at[me], lambda i: stats.at[i], st_s, st_r)
    st_gather.start()

    mine = 2 * p.diag
    own_set = mine + p.core
    slots = [own_set * 4 + j for j in range(4)]
    for slot in slots:
        gw_buf[slot] = jnp.zeros((DIM, CHUNK), F32)

    def backward(i, _):
        lo = pl.multiple_of(i * 512, 512)
        dz = grad_logits(zs[pl.ds(lo, 512), :], stats, me, lab_own, lo)
        part = dot_nn(w_out[:, pl.ds(lo, 512)], dz)
        for j, slot in enumerate(slots):
            gw_buf[slot] += part[:, j * CHUNK:(j + 1) * CHUNK]
        return 0

    lax.fori_loop(0, OCT, backward, 0, unroll=2)
    sums = None
    for j, slot in enumerate(slots):
        cols = slice(j * CHUNK, (j + 1) * CHUNK)
        h32 = ht[me, :, cols].astype(F32)
        dp = (gw_buf[slot] * (1.0 - h32 * h32)).astype(BF16)
        part = dot_nt(dp, sel[:, cols])
        sums = part if sums is None else sums + part
    da_all[me] = sums[:, 0:TILE].astype(BF16)
    dc_all[me] = jnp.concatenate([sums[0:MID, TILE:WIDE], sums[MID:DIM, TILE:WIDE]], axis=1)
    da_relay = Relay(p, lambda e: da_all.at[e], lambda e, h: da_all.at[e, h * MID:(h + 1) * MID, :], da_s, da_r)
    dc_relay = Relay(p, lambda e: dc_all.at[e], lambda e, h: dc_all.at[e, h * 160:(h + 1) * 160, :], dc_s, dc_r)
    da_relay.start()
    dc_relay.start()

    f_relay.finish()
    for k in range(1, N_DEV):
        hidden(lax.rem(me + k, N_DEV), k % 2)
    st_gather.wait_recv()
    pair = Pair(p, gw_buf, mine, 2 - mine, gw_s, gw_r)

    def chunk(c, _):
        n = own_set * 4 + c
        first = pl.multiple_of(n * CHUNK, CHUNK)
        rows = wt[pl.ds(first, CHUNK), :]
        z = dot_nn(rows, ht[0])
        for d in range(N_DEV):
            z_next = dot_nn(rows, ht[d + 1]) if d + 1 < N_DEV else None
            dz = grad_logits(z, stats, d, lab[d:d + 1, :], first)
            part = dot_nt(ht[d], dz)
            gw_buf[n] = part if d == 0 else gw_buf[n] + part
            z = z_next
        pair.start(c)

        @pl.when(c == 0)
        def _():
            da_relay.pass_on()
            dc_relay.pass_on()

        @pl.when(c == 1)
        def _():
            da_relay.pass_diagonal()
            dc_relay.pass_diagonal()

        @pl.when(c >= 2)
        def _():
            pair.pass_on(c - 2)

        return 0

    lax.fori_loop(0, 4, chunk, 0)
    da_relay.finish()
    dc_relay.finish()

    total = jnp.zeros((1, TILE), F32)
    for d in range(N_DEV):
        own = jnp.where(iota((1, TILE), 1) < OCT, stats[d, DIAGS:25, :], 0.0)
        total = total - (pltpu.roll(own, OCT * d, 1) if d else own)
    loss[...] = total[:, 0:HALF]

    def flip(x):
        width = x.shape[0]
        return jnp.concatenate([dot_nt(ident[:min(CHUNK, DIM - lo), :min(CHUNK, DIM - lo)], x[:, lo:lo + CHUNK]).astype(BF16)
                                for lo in range(0, DIM, CHUNK)], axis=0)

    for d in range(0, N_DEV, 2):
        fs = jnp.concatenate([f_all[d], f_all[d + 1]], axis=0)
        das = jnp.concatenate([da_all[d], da_all[d + 1]], axis=1)
        part = dot_nt(flip(fs), das)
        gw_enc[...] = part if d == 0 else gw_enc[...] + part
    for d in range(0, N_DEV, 4):
        dcs = jnp.concatenate([jnp.concatenate([dc_all[d + i, :, 0:HALF], dc_all[d + i, :, HALF:TILE]], axis=0)
                               for i in range(4)], axis=1).astype(BF16)
        part = dot_nt(flip(g[d * HALF:(d + 4) * HALF, :]), dcs)
        gw_pred[...] = part if d == 0 else gw_pred[...] + part
    pick = jnp.where(iota((16, TILE), 1) == iota((16, TILE), 0) + me * 16, 1.0, 0.0).astype(BF16)
    rows = jnp.concatenate([dot_nt(pick, da_all[d]).astype(BF16) for d in range(N_DEV)], axis=0)
    grad_enc[...] = dot_nt(rows, w_enc[...]).reshape(HALF, 2, DIM).astype(BF16)

    pair.pass_on(2)
    pair.pass_on(3)
    for c in range(4):
        pair.finish(c)
    for copy in copies:
        copy.wait_send()
    st_gather.wait_send()


def flush_kernel(loss, grad_enc, gw_enc, gw_pred, gw_buf, loss_out, grad_enc_out, gw_enc_out, gw_pred_out, gw_out, out_sem):
    moves = [(gw_buf.at[n], gw_out.at[:, n * CHUNK:(n + 1) * CHUNK]) for n in range(VOCAB // CHUNK)]
    moves += [(loss, loss_out), (grad_enc, grad_enc_out), (gw_enc, gw_enc_out), (gw_pred, gw_pred_out)]
    moves = [pltpu.make_async_copy(src, dst, out_sem.at[k]) for k, (src, dst) in enumerate(moves)]
    for copy in moves:
        copy.start()
    for copy in moves:
        copy.wait()


def vmem():
    return pl.BlockSpec(memory_space=pltpu.VMEM)


def solution(mesh):
    dma = pltpu.SemaphoreType.DMA

    def local_fn(enc_out, pred_out, w_enc, w_pred, w_out, labels, frame_len, label_len):
        n_utt = pred_out.shape[0]
        g = pred_out.reshape(OCT * n_utt, DIM)
        hbm = pl.BlockSpec(memory_space=pl.ANY)
        mem = pltpu.VMEM
        outs = [((1, n_utt), F32), (enc_out.shape, BF16), ((DIM, DIM), F32), ((DIM, DIM), F32)]
        handed = pl.pallas_call(
            main_kernel,
            out_shape=tuple(mem(shape, kind) for shape, kind in outs + [((16, DIM, CHUNK), F32)]),
            in_specs=[vmem()] + [hbm] * 4 + [vmem()] * 3,
            out_specs=(vmem(),) * 5,
            scratch_shapes=[mem((TILE, DIM), BF16), mem((512, DIM), BF16), mem((DIM, DIM), BF16), mem((DIM, VOCAB), BF16),
                            mem((VOCAB, DIM), BF16), mem((OCT, DIM, LANES), BF16), mem((VOCAB, LANES), F32),
                            mem((WIDE, LANES), BF16), mem((2, DIM, WIDE), BF16), mem((OCT, DIM, HALF), BF16), mem((DIM, DIM), BF16),
                            mem((OCT, DIM, TILE), BF16), mem((OCT, MID, TILE), F32), mem((OCT, TILE, DIM), BF16),
                            mem((OCT, 32, TILE), F32), mem((2, 40, TILE), F32), mem((OCT, TILE), jnp.int32),
                            mem((OCT, TILE), jnp.int32), mem((1, TILE), jnp.int32), dma((7,))]
            + [dma((OCT,))] * 4 + [dma((4, 5))] * 2 + [dma((9,))] * 6,
            compiler_params=pltpu.CompilerParams(collective_id=0, has_side_effects=True, vmem_limit_bytes=MAIN_VMEM),
        )(enc_out, g, w_enc, w_pred, w_out, labels.T, frame_len.reshape(1, n_utt), label_len.reshape(1, n_utt))
        outs.append(((DIM, VOCAB), F32))
        loss, grad_enc, gw_enc, gw_pred, gw_out = pl.pallas_call(
            flush_kernel,
            out_shape=tuple(jax.ShapeDtypeStruct(shape, kind) for shape, kind in outs),
            in_specs=[vmem()] * 5,
            out_specs=(hbm,) * 5,
            scratch_shapes=[dma((20,))],
            compiler_params=pltpu.CompilerParams(vmem_limit_bytes=LAST_VMEM),
        )(*handed)
        return loss.reshape(n_utt), grad_enc, gw_enc, gw_pred, gw_out

    in_specs = (P('dp', 'seq', None), P('dp', None, None), P(None, None), P(None, None), P(None, None), P('dp', None), P('dp'), P('dp'))
    out_specs = (P('dp'), P('dp', 'seq', None), P('dp', None), P('dp', None), P('dp', None))
    return jax.shard_map(local_fn, mesh=mesh, in_specs=in_specs, out_specs=out_specs, check_vma=False)
```

time: 96.5 us -> 85.5 us (0.89)
  Pallas kernels: 95.5 us -> 84.6 us
    pallas_call x2, Pallas kernels: 95.5 us -> 84.6 us  [the longest x1 79.4 us: local_fn(): pl.pallas_call(main_kernel, out_shape=tuple((mem(shape, kind) for shape,...]
where the time goes in v3:
time: 85.5 us; the launch traced here: 85.4 us
  Pallas kernels  84.6 us (99%)
    pallas_call x1, Pallas kernels, local_fn(): pl.pallas_call(main_kernel, out_shape=tuple((mem(shape, kind) for shape,...  79.4 us
    pallas_call x1, Pallas kernels, local_fn(): pl.pallas_call(flush_kernel, out_shape=tuple((jax.ShapeDtypeStruct(shape,...  5.17 us

profile of v3, /device:TPU:0, one launch (start us, length us, event | category | flops | bytes accessed | tf_op | source)
XLA Modules:
  0.0 85.4 jit_solution(12810353790469216618)
XLA Ops:
  0.6 79.4 %shard_map.119 = (f32[1,64]{1,0:T(1,128)S(1)}, bf16[64,2,640]{2,1,0:T(2,128)(2,1)S(1)}, f32[640,640]{1,0:T(8,128)S(1)}, f32[640,640]{1,0:T(8,128)S(1)}, f32[16,640,256]{2,1,0:T(8,128)S(1)}) custom-call(bf16[64,2,640]{2,1,0:T(2,128)(2,1)} %enc3.1, bf16[512,640]{1,0:T(8,128)(2,1)} %bitcast.5, bf16[640,640]{1,0:T(8,128)(2,1)} %we_hbm.1, ...), custom_call_target="tpu_custom_call" | custom-call | tf_op jit(solution)/shard_map/pallas_call | solution.py:533
  80.0 5.2 %shard_map.120 = (f32[1,64]{1,0:T(1,128)}, bf16[64,2,640]{2,1,0:T(2,128)(2,1)}, f32[640,640]{1,0:T(8,128)}, f32[640,640]{1,0:T(8,128)}, f32[640,4096]{1,0:T(8,128)}) custom-call(f32[1,64]{1,0:T(1,128)S(1)} %get-tuple-element.15.loss, bf16[64,2,640]{2,1,0:T(2,128)(2,1)S(1)} %get-tuple-element.16.grad_enc, f32[640,640]{1,0:T(8,128)S(1)} %get-tuple-element.17.gw_enc, ...), custom_call_target="tpu_custom_call" | custom-call | tf_op jit(solution)/shard_map/pallas_call | solution.py:548

commit v4 on v3

--- a/solution.py
+++ b/solution.py
@@ -13,7 +13,7 @@
 VOCAB = 4096
 LANES = 1024
 CHUNK = 256
-MAIN_VMEM = 52_600_000
+MAIN_VMEM = 53_000_000
 LAST_VMEM = 1_000_000
 OCT, DIAGS, HALF, TILE, WIDE, MID = 8, 24, 64, 128, 192, 320
 
@@ -298,7 +298,7 @@
 
 def main_kernel(enc3, g_hbm, we_hbm, wp_hbm, w_hbm, labels, frame_len, label_len,
                 loss, grad_enc, gw_enc, gw_pred, gw_buf,
-                enc, g, w_enc, w_out, wt, ht, zs, sel, act, c_all, wet, da_all, dc_all, f_all, stats, skew, lab, lab_x, len_x,
+                enc, g, w_out, wt, ht, zs, sel, act, c_all, wet, da_all, dc_all, f_all, stats, skew, lab, lab_x, len_x,
                 load_sem, a2a_s, a2a_r, st_s, st_r, gw_s, gw_r, f_s, f_r, da_s, da_r, dc_s, dc_r):
     p = Peers()
     me = p.me
@@ -306,7 +306,7 @@
     for k in range(1, N_DEV):
         pl.semaphore_signal(barrier, inc=1, device_id=p.target(lax.rem(me + k, N_DEV)),
                             device_id_type=pl.DeviceIdType.MESH)
-    w_pred, wpt = ht.at[0, :, 0:DIM], ht.at[1, :, 0:DIM]
+    w_pred, wpt, w_enc = ht.at[0, :, 0:DIM], ht.at[1, :, 0:DIM], ht.at[2, :, 0:DIM]
     loads = [(wp_hbm, w_pred), (g_hbm, g), (we_hbm, w_enc)]
     for lo in range(0, VOCAB, LANES):
         loads.append((w_hbm.at[:, lo:lo + LANES], w_out.at[:, lo:lo + LANES]))
@@ -348,8 +348,8 @@
     transpose_into(wpt, w_pred, ident)
     transpose_into(wet, w_enc, ident)
     c_cols = dot_nt(wpt[...], g[...]).astype(BF16)
-    for d in range(N_DEV):
-        c_all[d] = c_cols[:, d * HALF:(d + 1) * HALF]
+    for k in range(4):
+        c_all[k] = c_cols[:, k * TILE:(k + 1) * TILE]
 
     def transpose_out(c, _):
         lo = pl.multiple_of(c * CHUNK, CHUNK)
@@ -369,7 +369,8 @@
 
     def hidden(d, slot):
         act[slot, :, 0:TILE] = dot_nt(wet[...], f_all[d]).astype(BF16)
-        act[slot, :, TILE:WIDE] = c_all[d]
+        two = c_all[d // 2]
+        act[slot, :, TILE:WIDE] = jnp.where(lax.rem(d, 2) == 1, two[:, HALF:TILE], two[:, 0:HALF])
         ht[d] = jnp.tanh(dot_nn(act[slot], sel[...])).astype(BF16)
 
     hidden(me, 0)
@@ -389,9 +390,9 @@
         return new, total, z_lab
 
     carry = (jnp.full((OCT, LANES), NEG, F32), jnp.zeros((OCT, LANES), F32), jnp.zeros((OCT, LANES), F32))
-    carry = lax.fori_loop(0, OCT, forward, carry, unroll=4)
+    carry = lax.fori_loop(0, OCT, forward, carry, unroll=8)
     f_relay.pass_on()
-    top, total, z_lab = lax.fori_loop(OCT, 16, forward, carry, unroll=4)
+    top, total, z_lab = lax.fori_loop(OCT, 16, forward, carry, unroll=8)
     f_relay.pass_diagonal()
     peak = jnp.max(top, axis=0, keepdims=True)
     lse = peak + jnp.log(jnp.sum(total * jnp.exp(top - peak), axis=0, keepdims=True))
@@ -404,6 +405,10 @@
     lattice(tiles(lse), tiles(z_blank), tiles(z_lab), n_frames, n_labels, me, skew, stats)
     st_gather = Direct(p, lambda d: stats.at[me], lambda i: stats.at[i], st_s, st_r)
     st_gather.start()
+
+    f_relay.finish()
+    for k in range(1, N_DEV):
+        hidden(lax.rem(me + k, N_DEV), k % 2)
 
     mine = 2 * p.diag
     own_set = mine + p.core
@@ -419,7 +424,7 @@
             gw_buf[slot] += part[:, j * CHUNK:(j + 1) * CHUNK]
         return 0
 
-    lax.fori_loop(0, OCT, backward, 0, unroll=2)
+    lax.fori_loop(0, OCT, backward, 0, unroll=4)
     sums = None
     for j, slot in enumerate(slots):
         cols = slice(j * CHUNK, (j + 1) * CHUNK)
@@ -434,9 +439,6 @@
     da_relay.start()
     dc_relay.start()
 
-    f_relay.finish()
-    for k in range(1, N_DEV):
-        hidden(lax.rem(me + k, N_DEV), k % 2)
     st_gather.wait_recv()
     pair = Pair(p, gw_buf, mine, 2 - mine, gw_s, gw_r)
 
@@ -453,12 +455,12 @@
             z = z_next
         pair.start(c)
 
-        @pl.when(c == 0)
+        @pl.when(c == 1)
         def _():
             da_relay.pass_on()
             dc_relay.pass_on()
 
-        @pl.when(c == 1)
+        @pl.when(c == 2)
         def _():
             da_relay.pass_diagonal()
             dc_relay.pass_diagonal()
@@ -496,7 +498,7 @@
         gw_pred[...] = part if d == 0 else gw_pred[...] + part
     pick = jnp.where(iota((16, TILE), 1) == iota((16, TILE), 0) + me * 16, 1.0, 0.0).astype(BF16)
     rows = jnp.concatenate([dot_nt(pick, da_all[d]).astype(BF16) for d in range(N_DEV)], axis=0)
-    grad_enc[...] = dot_nt(rows, w_enc[...]).reshape(HALF, 2, DIM).astype(BF16)
+    grad_enc[...] = dot_nn(rows, wet[...]).reshape(HALF, 2, DIM).astype(BF16)
 
     pair.pass_on(2)
     pair.pass_on(3)
@@ -535,9 +537,9 @@
             out_shape=tuple(mem(shape, kind) for shape, kind in outs + [((16, DIM, CHUNK), F32)]),
             in_specs=[vmem()] + [hbm] * 4 + [vmem()] * 3,
             out_specs=(vmem(),) * 5,
-            scratch_shapes=[mem((TILE, DIM), BF16), mem((512, DIM), BF16), mem((DIM, DIM), BF16), mem((DIM, VOCAB), BF16),
+            scratch_shapes=[mem((TILE, DIM), BF16), mem((512, DIM), BF16), mem((DIM, VOCAB), BF16),
                             mem((VOCAB, DIM), BF16), mem((OCT, DIM, LANES), BF16), mem((VOCAB, LANES), F32),
-                            mem((WIDE, LANES), BF16), mem((2, DIM, WIDE), BF16), mem((OCT, DIM, HALF), BF16), mem((DIM, DIM), BF16),
+                            mem((WIDE, LANES), BF16), mem((2, DIM, WIDE), BF16), mem((4, DIM, TILE), BF16), mem((DIM, DIM), BF16),
                             mem((OCT, DIM, TILE), BF16), mem((OCT, MID, TILE), F32), mem((OCT, TILE, DIM), BF16),
                             mem((OCT, 32, TILE), F32), mem((2, 40, TILE), F32), mem((OCT, TILE), jnp.int32),
                             mem((OCT, TILE), jnp.int32), mem((1, TILE), jnp.int32), dma((7,))]

time: 85.5 us -> 83.8 us (0.980)
  Pallas kernels: 84.6 us -> 82.8 us
    pallas_call x1, Pallas kernels: 79.4 us -> 77.7 us  [local_fn(): pl.pallas_call(main_kernel, out_shape=tuple((mem(shape, kind) for shape,...]
where the time goes in v4:
time: 83.8 us; the launch traced here: 83.6 us
  Pallas kernels  82.8 us (99%)
    pallas_call x1, Pallas kernels, local_fn(): pl.pallas_call(main_kernel, out_shape=tuple((mem(shape, kind) for shape,...  77.7 us
    pallas_call x1, Pallas kernels, local_fn(): pl.pallas_call(flush_kernel, out_shape=tuple((jax.ShapeDtypeStruct(shape,...  5.17 us

profile of v4, /device:TPU:0, one launch (start us, length us, event | category | flops | bytes accessed | tf_op | source)
XLA Modules:
  0.0 83.6 jit_solution(11910527713631227119)
XLA Ops:
  0.6 77.7 %shard_map.119 = (f32[1,64]{1,0:T(1,128)S(1)}, bf16[64,2,640]{2,1,0:T(2,128)(2,1)S(1)}, f32[640,640]{1,0:T(8,128)S(1)}, f32[640,640]{1,0:T(8,128)S(1)}, f32[16,640,256]{2,1,0:T(8,128)S(1)}) custom-call(bf16[64,2,640]{2,1,0:T(2,128)(2,1)} %enc3.1, bf16[512,640]{1,0:T(8,128)(2,1)} %bitcast.5, bf16[640,640]{1,0:T(8,128)(2,1)} %we_hbm.1, ...), custom_call_target="tpu_custom_call" | custom-call | tf_op jit(solution)/shard_map/pallas_call | solution.py:535
  78.3 5.2 %shard_map.120 = (f32[1,64]{1,0:T(1,128)}, bf16[64,2,640]{2,1,0:T(2,128)(2,1)}, f32[640,640]{1,0:T(8,128)}, f32[640,640]{1,0:T(8,128)}, f32[640,4096]{1,0:T(8,128)}) custom-call(f32[1,64]{1,0:T(1,128)S(1)} %get-tuple-element.15.loss, bf16[64,2,640]{2,1,0:T(2,128)(2,1)S(1)} %get-tuple-element.16.grad_enc, f32[640,640]{1,0:T(8,128)S(1)} %get-tuple-element.17.gw_enc, ...), custom_call_target="tpu_custom_call" | custom-call | tf_op jit(solution)/shard_map/pallas_call | solution.py:550
